TPU v7x, 32 devices: a whole 2x2x4 slice. The times are simulated.
32 devices in a mesh: frame: 16 (over z, y, x), row: 2 (over core).
Axes of the slice: x: 2, y: 2, z: 4, core: 2. Of those that a mesh axis runs over, the one named last changes fastest.
Arguments:
- footage: float32 [64, 1024, 1024], P('frame', 'row'), may hold values from -30 to 30
Outputs:
- coefficients: float32 [64, 1024, 1024], P('frame', 'row')
- energies: float32 [4, 10], replicated
All inputs are finite; a program needn't handle non-finite values.
Results may differ from a plain program's by a relative error of at most 0.00007.
Values sent between devices are 32-bit elements; how exact they have to be, the bound alone decides.
A program may use at most 128 MiB of HBM per device.

v0:
```python
import functools

import jax
import jax.numpy as jnp
import numpy as np
from jax import lax
from jax.experimental import pallas as pl
from jax.experimental.pallas import tpu as pltpu
from jax.sharding import PartitionSpec as P

SLEVELS = 3
TLEVELS = 3
PERIOD = 2**SLEVELS
MARGIN = 4
GROUP = 4

LIFT_ALPHA = -1.586134342
LIFT_BETA = -0.05298011854
LIFT_GAMMA = 0.8829110762
LIFT_DELTA = 0.4435068522
LIFT_ZETA = 1.149604398
STEPS = (LIFT_ALPHA, LIFT_BETA, LIFT_GAMMA, LIFT_DELTA)
REACH = 4
TAPS = 2 * REACH + 1
MASKS = TAPS * SLEVELS
MESH = pl.DeviceIdType.MESH


def level_of(number, ceiling):
    depth_now = 1
    while number % 2 == 0 and depth_now <= ceiling:
        number = number // 2
        depth_now = depth_now + 1
    return depth_now


def space_table(levels):
    period = 2**levels
    band_table = np.zeros((period * period, 3 * levels + 1), np.float32)
    for row_pos in range(period):
        for col_pos in range(period):
            row_level = level_of(row_pos, levels)
            col_level = level_of(col_pos, levels)
            finest = min(row_level, col_level)
            if finest > levels:
                column = 3 * levels
            elif row_level == col_level:
                column = 3 * (finest - 1) + 2
            elif row_level == finest:
                column = 3 * (finest - 1)
            else:
                column = 3 * (finest - 1) + 1
            band_table[row_pos * period + col_pos, column] = 1.0
    return band_table


def time_table(levels):
    period = 2**levels
    band_table = np.zeros((period, levels + 1), np.float32)
    for number in range(period):
        band_table[number, level_of(number, levels) - 1] = 1.0
    return band_table


def band_means(totals, frames_all, rows_all, cols_all, levels_s, levels_t):
    space_share = space_table(levels_s).sum(0) / float((2**levels_s) ** 2)
    time_share = time_table(levels_t).sum(0) / float(2**levels_t)
    counts = (
        float(frames_all) * float(rows_all) * float(cols_all) * np.outer(time_share, space_share)
    )
    return totals / jnp.asarray(counts, jnp.float32)


def shifted(block, axis, distance):
    devices = range(lax.axis_size(axis))
    route = [(i - distance, i) for i in devices if i - distance in devices]
    return lax.ppermute(block, axis, route)


def lifted_identity(size):
    x = np.eye(size)
    after = np.concatenate([np.arange(2, size, 2), [size - 2]])
    before = np.concatenate([[1], np.arange(1, size - 1, 2)])
    even, odd = np.arange(0, size, 2), np.arange(1, size, 2)
    x[:, odd] += LIFT_ALPHA * (x[:, even] + x[:, after])
    x[:, even] += LIFT_BETA * (x[:, before] + x[:, odd])
    x[:, odd] += LIFT_GAMMA * (x[:, even] + x[:, after])
    x[:, even] += LIFT_DELTA * (x[:, before] + x[:, odd])
    x[:, even] *= LIFT_ZETA
    x[:, odd] *= 1.0 / LIFT_ZETA
    return x


def lane_table(width):
    table = np.zeros((MASKS + SLEVELS, width), np.float64)
    for level in range(SLEVELS):
        s = 2**level
        size = width // s
        matrix = lifted_identity(size)
        table[TAPS * level + REACH] = 1.0
        for k in range(-REACH, REACH + 1):
            n = np.arange(max(0, -k), min(size, size - k))
            row = np.zeros(size)
            row[n] = matrix[n + k, n]
            table[TAPS * level + REACH + k, ::s] = row
        table[MASKS + level, ::s] = 1.0
    return table.astype(np.float32)


def spatial_frame(frame, frames, tab_ref, x_ref, halo_ref, o_ref, xin, buf, x_sem, h_sem):
    groups, width = buf.shape[1:]
    inner = groups - 2 * MARGIN
    row = lax.axis_index("row")
    at_top = row == 0
    at_bottom = row == lax.axis_size("row") - 1
    slot = frame % 2

    def copies(f, slot):
        for p in range(PERIOD):
            yield pltpu.make_async_copy(
                x_ref.at[f, :, p, :], xin.at[slot, p, pl.ds(0, inner), :], x_sem.at[slot, p]
            )
            yield pltpu.make_async_copy(
                halo_ref.at[f, p], xin.at[slot, p, pl.ds(inner, 2 * MARGIN), :], h_sem.at[slot, p]
            )

    @pl.when(frame == 0)
    def _():
        for copy in copies(frame, slot):
            copy.start()

    @pl.when(frame + 1 < frames)
    def _():
        for copy in copies(frame + 1, 1 - slot):
            copy.start()

    for copy in copies(frame, slot):
        copy.wait()

    tile = 24
    tiles = groups // tile
    for level in range(SLEVELS):
        s = 2**level
        source = xin.at[slot] if level == 0 else buf

        def columns(i, carry, level=level, s=s, source=source):
            phase = (i // tiles) * s
            q = pl.ds(pl.multiple_of((i % tiles) * tile, 8), tile)
            x = source[phase, q, :]
            y = x * tab_ref[pl.ds(TAPS * level + REACH, 1), :]
            for k in range(1, REACH + 1):
                for sign in (-1, 1):
                    moved = pltpu.roll(x, (-sign * k * s) % width, 1)
                    y = y + moved * tab_ref[pl.ds(TAPS * level + REACH + sign * k, 1), :]
            buf[phase, q, :] = y
            return carry

        lax.fori_loop(0, (PERIOD // s) * tiles, columns, 0)

        def rows(i, carry, level=level, s=s):
            lanes = pl.ds(pl.multiple_of(i * 128, 128), 128)
            mask = tab_ref[pl.ds(MASKS + level, 1), lanes]
            x = {p: buf[p, :, lanes] for p in range(0, PERIOD, s)}
            index = lax.broadcasted_iota(jnp.int32, (groups, 128), 0)
            first = jnp.logical_and(index == 0, at_top)
            last = jnp.logical_and(index == inner - 1, at_bottom)
            for step, factor in enumerate(STEPS):
                c = factor * mask
                if step % 2 == 0:
                    for p in range(s, PERIOD, 2 * s):
                        if p + s < PERIOD:
                            after = x[p + s]
                        else:
                            after = jnp.where(last, x[p - s], pltpu.roll(x[0], groups - 1, 0))
                        x[p] = x[p] + c * (x[p - s] + after)
                else:
                    for p in range(0, PERIOD, 2 * s):
                        if p > 0:
                            before = x[p - s]
                        else:
                            before = jnp.where(first, x[s], pltpu.roll(x[PERIOD - s], 1, 0))
                        x[p] = x[p] + c * (before + x[p + s])
            up = jnp.where(mask > 0, LIFT_ZETA, 1.0)
            down = jnp.where(mask > 0, 1.0 / LIFT_ZETA, 1.0)
            for p in x:
                low = p % (2 * s) == 0
                value = x[p] * (up if low else down)
                if low and level < SLEVELS - 1:
                    buf[p, :, lanes] = value
                else:
                    o_ref[frame, p, :, lanes] = value[:inner]
            return carry

        lax.fori_loop(0, width // 128, rows, 0)


def outgoing(f):
    o = {i: f[i] - 0.5 * (f[i - 1] + f[i + 1]) for i in range(1, 14, 2)}
    a = {i: f[i] + 0.25 * (o[i - 1] + o[i + 1]) for i in range(2, 13, 2)}
    p6 = a[6] - 0.5 * (a[4] + a[8])
    p10 = a[10] - 0.5 * (a[8] + a[12])
    b8 = a[8] + 0.25 * (p6 + p10)
    to_before = (f[0], o[1], a[2] - 0.5 * a[4])
    to_after = (
        f[15] - 0.5 * f[14],
        f[14] + 0.25 * o[13] - 0.5 * a[12],
        a[12] + 0.25 * p10 - 0.5 * b8,
    )
    return to_before, to_after


def temporal(f, before, after, is_first, is_last):
    o = {i: f[i] - 0.5 * (f[i - 1] + f[i + 1]) for i in range(1, 14, 2)}
    f16 = jnp.where(is_last, f[14], after[0])
    o[15] = f[15] - 0.5 * (f[14] + f16)
    o[-1] = jnp.where(is_first, o[1], before[0] - 0.5 * f[0])
    a = {i: f[i] + 0.25 * (o[i - 1] + o[i + 1]) for i in range(0, 16, 2)}
    a16 = jnp.where(is_last, a[12], after[0] + 0.25 * (o[15] + after[1]))
    a[16] = a16
    p = {i: a[i] - 0.5 * (a[i - 2] + a[i + 2]) for i in range(2, 16, 4)}
    p[-2] = jnp.where(is_first, p[2], before[1] + 0.25 * o[-1] - 0.5 * a[0])
    b = {i: a[i] + 0.25 * (p[i - 2] + p[i + 2]) for i in range(0, 16, 4)}
    b[16] = jnp.where(is_last, b[8], a16 + 0.25 * (p[14] + after[2] - 0.5 * a16))
    d4 = b[4] - 0.5 * (b[0] + b[8])
    d12 = b[12] - 0.5 * (b[8] + b[16])
    dm4 = jnp.where(is_first, d4, before[2] + 0.25 * p[-2] - 0.5 * b[0])
    out = {i: o[i] for i in range(1, 16, 2)}
    out.update({i: p[i] for i in range(2, 16, 4)})
    out[4], out[12] = d4, d12
    out[0] = b[0] + 0.25 * (dm4 + d4)
    out[8] = b[8] + 0.25 * (d4 + d12)
    return out


def video_kernel(tab_ref, x_ref, halo_ref, o_ref, sums_ref, xin, buf, planes, mine, held,
                 from_before, from_after, to_before, to_after, x_sem, e_sem,
                 f_send, f_recv, f_own, h_send, h_recv, r_send, r_recv, r_own, m_own):
    frames, phases, inner, width = planes.shape
    part = inner // GROUP
    inside = [n for n in range(1, frames - 1, 2)]
    moved = [n for n in range(frames) if n not in inside]
    me = lax.axis_index("frame")
    count = lax.axis_size("frame")
    member = me % GROUP
    base = me - member
    is_first = base == 0
    is_last = base == count - GROUP
    previous = (me + count - GROUP) % count
    following = (me + GROUP) % count
    peers = [base + (member + k) % GROUP for k in range(1, GROUP)]

    barrier = pltpu.get_barrier_semaphore()
    for peer in peers + [previous, following]:
        pl.semaphore_signal(barrier, inc=1, device_id={"frame": peer}, device_id_type=MESH)
    pl.semaphore_wait(barrier, GROUP + 1)

    def part_of(device):
        return pl.ds(pl.multiple_of((device % GROUP) * part, 8), part)

    def spot(device, n):
        return (device % GROUP) * frames + n

    def forward(n, c, k):
        peer = peers[k]
        return pltpu.make_async_remote_copy(
            src_ref=planes.at[n, c, part_of(peer), :],
            dst_ref=held.at[spot(me, n), c],
            send_sem=f_send.at[n, k, c],
            recv_sem=f_recv.at[n, k, c],
            device_id={"frame": peer},
            device_id_type=MESH,
        )

    def forward_own(n, c):
        return pltpu.make_async_copy(
            planes.at[n, c, part_of(me), :], held.at[spot(me, n), c], f_own.at[n, c]
        )

    def halo(c, side):
        return pltpu.make_async_remote_copy(
            src_ref=(to_before if side == 0 else to_after).at[c],
            dst_ref=(from_after if side == 0 else from_before).at[c],
            send_sem=h_send.at[side, c],
            recv_sem=h_recv.at[side, c],
            device_id={"frame": previous if side == 0 else following},
            device_id_type=MESH,
        )

    def back(i, c, k):
        peer = peers[k]
        return pltpu.make_async_remote_copy(
            src_ref=held.at[spot(peer, moved[i]), c],
            dst_ref=o_ref.at[moved[i], c, part_of(me), :],
            send_sem=r_send.at[i, k, c],
            recv_sem=r_recv.at[i, k, c],
            device_id={"frame": peer},
            device_id_type=MESH,
        )

    def back_own(i, c):
        return pltpu.make_async_copy(
            held.at[spot(me, moved[i]), c], o_ref.at[moved[i], c, part_of(me), :], r_own.at[i, c]
        )

    def keep(i, c):
        return pltpu.make_async_copy(mine.at[i, c], o_ref.at[inside[i], c], m_own.at[i, c])

    def one_frame(n, carry):
        spatial_frame(n, frames, tab_ref, x_ref, halo_ref, planes, xin, buf, x_sem, e_sem)

        def start_forward(c, carry):
            for k in range(GROUP - 1):
                forward(n, c, k).start()
            forward_own(n, c).start()
            return carry

        return lax.fori_loop(0, phases, start_forward, carry)

    lax.fori_loop(0, frames, one_frame, 0)

    def inside_highs(c, carry):
        for i, n in enumerate(inside):
            mine[i, c] = planes[n, c] - 0.5 * (planes[n - 1, c] + planes[n + 1, c])
            keep(i, c).start()
        return carry

    lax.fori_loop(0, phases, inside_highs, 0)
    total = GROUP * frames
    strip = 128
    strips = width // strip

    def send_halo(c):
        for n in range(frames):
            for k in range(GROUP - 1):
                forward(n, c, k).wait_recv()
            forward_own(n, c).wait()

        def tile(i, carry):
            lanes = pl.ds(pl.multiple_of(i * strip, strip), strip)
            left, right = outgoing([held[n, c, :, lanes] for n in range(total)])
            for j in range(TLEVELS):
                to_before[c, j, :, lanes] = left[j]
                to_after[c, j, :, lanes] = right[j]
            return carry

        lax.fori_loop(0, strips, tile, 0)
        for side in range(2):
            halo(c, side).start()

    def finish(c):
        for side in range(2):
            halo(c, side).wait_recv()

        def tile(i, carry):
            lanes = pl.ds(pl.multiple_of(i * strip, strip), strip)
            f = [held[n, c, :, lanes] for n in range(total)]
            before = [from_before[c, j, :, lanes] for j in range(TLEVELS)]
            after = [from_after[c, j, :, lanes] for j in range(TLEVELS)]
            out = temporal(f, before, after, is_first, is_last)
            sums = [None] * (TLEVELS + 1)
            for n in range(total):
                if n % frames in moved:
                    held[n, c, :, lanes] = out[n]
                t = level_of(n % 2**TLEVELS, TLEVELS) - 1
                square = out[n] * out[n]
                sums[t] = square if sums[t] is None else sums[t] + square
            for t in range(TLEVELS + 1):
                sums_ref[t, c, :, lanes] = jnp.sum(
                    sums[t].reshape(part // 8, 8, strip), axis=0
                )
            return carry

        lax.fori_loop(0, strips, tile, 0)
        for i in range(len(moved)):
            for k in range(GROUP - 1):
                back(i, c, k).start()
            back_own(i, c).start()

    send_halo(0)

    def middle(c, carry):
        send_halo(c)
        finish(c - 1)
        return carry

    lax.fori_loop(1, phases, middle, 0)
    finish(phases - 1)

    def drain(c, carry):
        for k in range(GROUP - 1):
            for n in range(frames):
                forward(n, c, k).wait_send()
            for i in range(len(moved)):
                back(i, c, k).wait()
        for side in range(2):
            halo(c, side).wait_send()
        for i in range(len(moved)):
            back_own(i, c).wait()
        for i in range(len(inside)):
            keep(i, c).wait()
        return carry

    lax.fori_loop(0, phases, drain, 0)


def transformed(footage):
    frames, rows, width = footage.shape
    edge = MARGIN * PERIOD
    inner = rows // PERIOD
    groups = inner + 2 * MARGIN
    part = inner // GROUP
    above = shifted(footage[:, -edge:], "row", 1)
    below = shifted(footage[:, :edge], "row", -1)
    halo = jnp.concatenate([below, above], axis=1)
    halo = halo.reshape(frames, 2 * MARGIN, PERIOD, width).transpose(0, 2, 1, 3)
    table = jnp.asarray(lane_table(width))
    any_space = pl.BlockSpec(memory_space=pl.ANY)
    vmem = pl.BlockSpec(memory_space=pltpu.VMEM)
    halo_buffer = pltpu.VMEM((PERIOD, TLEVELS, part, width), jnp.float32)
    dma = pltpu.SemaphoreType.DMA
    kept = len(range(1, frames - 1, 2))
    sent = frames - kept
    return pl.pallas_call(
        video_kernel,
        out_shape=(
            jax.ShapeDtypeStruct((frames, PERIOD, inner, width), jnp.float32),
            jax.ShapeDtypeStruct((TLEVELS + 1, PERIOD, 8, width), jnp.float32),
        ),
        in_specs=[vmem, any_space, any_space],
        out_specs=(any_space, vmem),
        scratch_shapes=[
            pltpu.VMEM((2, PERIOD, groups, width), jnp.float32),
            pltpu.VMEM((PERIOD, groups, width), jnp.float32),
            pltpu.VMEM((frames, PERIOD, inner, width), jnp.float32),
            pltpu.VMEM((kept, PERIOD, inner, width), jnp.float32),
            pltpu.VMEM((GROUP * frames, PERIOD, part, width), jnp.float32),
            halo_buffer, halo_buffer, halo_buffer, halo_buffer,
            dma((2, PERIOD)), dma((2, PERIOD)),
            dma((frames, GROUP - 1, PERIOD)), dma((frames, GROUP - 1, PERIOD)),
            dma((frames, PERIOD)),
            dma((2, PERIOD)), dma((2, PERIOD)),
            dma((sent, GROUP - 1, PERIOD)), dma((sent, GROUP - 1, PERIOD)),
            dma((sent, PERIOD)), dma((kept, PERIOD)),
        ],
        compiler_params=pltpu.CompilerParams(
            collective_id=0, has_side_effects=True, vmem_limit_bytes=56 * 2**20
        ),
    )(table, footage.reshape(frames, inner, PERIOD, width), halo)


def total_kernel(x_ref, o_ref, inbox, send, recv):
    strips = lax.axis_size("row")
    count = lax.axis_size("frame") * strips
    me = lax.axis_index("frame") * strips + lax.axis_index("row")

    def place(device):
        return {"frame": device // strips, "row": device % strips}

    barrier = pltpu.get_barrier_semaphore()

    def greet(j, carry):
        pl.semaphore_signal(
            barrier, inc=1, device_id=place((me + j) % count), device_id_type=MESH
        )
        return carry

    lax.fori_loop(1, count, greet, 0)
    pl.semaphore_wait(barrier, count - 1)

    def to_peer(j):
        return pltpu.make_async_remote_copy(
            src_ref=x_ref,
            dst_ref=inbox.at[me],
            send_sem=send.at[j],
            recv_sem=recv.at[me],
            device_id=place((me + j) % count),
            device_id_type=MESH,
        )

    def start(j, carry):
        to_peer(j).start()
        return carry

    lax.fori_loop(1, count, start, 0)

    inbox[me] = x_ref[...]

    def arrive(j, carry):
        source = (me + j) % count
        pltpu.make_async_remote_copy(
            src_ref=x_ref,
            dst_ref=inbox.at[source],
            send_sem=send.at[j],
            recv_sem=recv.at[source],
            device_id=place(source),
            device_id_type=MESH,
        ).wait_recv()
        return carry

    lax.fori_loop(1, count, arrive, 0)
    o_ref[...] = lax.fori_loop(
        1, count, lambda j, total: total + inbox[j], inbox[0]
    )

    def drain(j, carry):
        to_peer(j).wait_send()
        return carry

    lax.fori_loop(1, count, drain, 0)


def total_over_devices(values):
    count = lax.axis_size("frame") * lax.axis_size("row")
    padded = jnp.zeros((8, 128), jnp.float32)
    padded = padded.at[: values.shape[0], : values.shape[1]].set(values)
    vmem = pl.BlockSpec(memory_space=pltpu.VMEM)
    total = pl.pallas_call(
        total_kernel,
        out_shape=jax.ShapeDtypeStruct((8, 128), jnp.float32),
        in_specs=[vmem],
        out_specs=vmem,
        scratch_shapes=[
            pltpu.VMEM((count, 8, 128), jnp.float32),
            pltpu.SemaphoreType.DMA((count,)),
            pltpu.SemaphoreType.DMA((count,)),
        ],
        compiler_params=pltpu.CompilerParams(collective_id=1, has_side_effects=True),
    )(padded)
    return total[: values.shape[0], : values.shape[1]]


def shards(footage):
    frames, rows, width = footage.shape
    coeffs, sums = transformed(footage)
    coeffs = coeffs.transpose(0, 2, 1, 3).reshape(frames, rows, width)
    pattern = sums.sum(axis=2).reshape(TLEVELS + 1, PERIOD, width // PERIOD, PERIOD).sum(axis=2)
    pattern = pattern.reshape(TLEVELS + 1, PERIOD * PERIOD)
    totals = jnp.dot(
        pattern, jnp.asarray(space_table(SLEVELS), jnp.float32), precision=lax.Precision.HIGHEST
    )
    totals = total_over_devices(totals)
    means = band_means(
        totals,
        frames * lax.axis_size("frame"),
        rows * lax.axis_size("row"),
        width,
        SLEVELS,
        TLEVELS,
    )
    return (coeffs, means)


def solution(mesh):
    return jax.shard_map(
        shards,
        mesh=mesh,
        in_specs=(P("frame", "row", None),),
        out_specs=(P("frame", "row", None), P()),
        check_vma=False,
    )
```

profile of v0, /device:TPU:0, one launch (start us, length us, event | category | flops | bytes accessed | tf_op | source)
XLA Modules:
  0.0 221.3 jit_solution(2367441440197192198)
XLA Ops:
  0.6 1.3 fusion
  1.9 1.3 collective-permute-start
  3.2 3.1 %collective-permute-start.1 = (f32[4,32,1024]{2,1,0:T(8,128)S(1)}, f32[4,32,1024]{2,1,0:T(8,128)S(1)}, u32[]{:S(2)}, u32[]{:S(2)}) collective-permute-start(f32[4,32,1024]{2,1,0:T(8,128)S(1)} %get-tuple-element.19), channel_id=1, source_target_pairs={{0,1},{2,3},{4,5},{6,7},{8,9},{10,11},{12,13},{14,15},{16,17},{18,... | collective-permute-start | bytes 1572872 | tf_op jit(solution)/shard_map/ppermute | solution.py:77
  6.3 0.0 collective-permute-done
  6.4 1.5 collective-permute-done.1
  7.8 0.1 maximum_bitcast_fusion
  7.9 1.6 copy.11
  9.5 186.5 %shard_map.59 = (f32[4,8,64,1024]{3,2,1,0:T(8,128)}, f32[4,8,8,1024]{3,2,1,0:T(8,128)}) custom-call(f32[30,1024]{1,0:T(8,128)} %constant.34.clone.tab_ref, f32[4,64,8,1024]{3,2,1,0:T(8,128)} %bitcast.12, f32[4,8,8,1024]{3,2,1,0:T(8,128)} %bitcast.15), custom_call_target="tpu_custom_call" | custom-call | tf_op jit(solution)/shard_map/pallas_call | solution.py:423
  196.1 0.0 copy-start
  196.1 0.0 copy-start.1
  196.1 0.0 copy-start.2
  196.1 11.7 %copy.10 = f32[4,64,8,1024]{3,2,1,0:T(8,128)} copy(f32[4,64,8,1024]{3,1,2,0:T(8,128)} %bitcast.14) | data formatting | bytes 16777216 | tf_op jit(solution)/shard_map/transpose | solution.py:535
  207.8 0.0 copy-done
  207.8 0.2 reduce_sum.18
  208.1 1.1 reshape.53
  209.2 0.2 reduce_sum.19
  209.4 0.1 reshape.54
  209.5 0.0 copy-done.1
  209.5 0.1 fusion.1
  209.6 0.6 scatter.4.x_ref
  210.2 9.8 %shard_map.60 = f32[8,128]{1,0:T(8,128)} custom-call(f32[8,128]{1,0:T(8,128)} %scatter.4.x_ref), custom_call_target="tpu_custom_call" | custom-call | tf_op jit(solution)/shard_map/pallas_call | solution.py:517
  220.0 0.0 copy-done.2
  220.1 1.3 slice_multiply_fusion
Async XLA Ops:
  1.9 4.4 %collective-permute-start = (f32[4,32,1024]{2,1,0:T(8,128)S(1)}, f32[4,32,1024]{2,1,0:T(8,128)S(1)}, u32[]{:S(2)}, u32[]{:S(2)}) collective-permute-start(f32[4,32,1024]{2,1,0:T(8,128)S(1)} %get-tuple-element.18), channel_id=1, source_target_pairs={{1,0},{3,2},{5,4},{7,6},{9,8},{11,10},{13,12},{15,14},{17,16},{19,... | collective-permute-start | bytes 1572872 | tf_op jit(solution)/shard_map/ppermute | solution.py:77
  3.2 4.6 %collective-permute-start.1 = (f32[4,32,1024]{2,1,0:T(8,128)S(1)}, f32[4,32,1024]{2,1,0:T(8,128)S(1)}, u32[]{:S(2)}, u32[]{:S(2)}) collective-permute-start(f32[4,32,1024]{2,1,0:T(8,128)S(1)} %get-tuple-element.19), channel_id=1, source_target_pairs={{0,1},{2,3},{4,5},{6,7},{8,9},{10,11},{12,13},{14,15},{16,17},{18,... | collective-permute-start | bytes 1572872 | tf_op jit(solution)/shard_map/ppermute | solution.py:77
  196.1 11.8 %copy-start = (f32[4,8,8,1024]{3,2,1,0:T(8,128)S(1)}, f32[4,8,8,1024]{3,2,1,0:T(8,128)}, u32[]{:S(2)}) copy-start(f32[4,8,8,1024]{3,2,1,0:T(8,128)} %get-tuple-element.17) | copy-start | bytes 3145732
  196.1 13.4 %copy-start.1 = (f32[64,10]{1,0:T(8,128)S(1)}, f32[64,10]{1,0:T(8,128)}, u32[]{:S(2)}) copy-start(f32[64,10]{1,0:T(8,128)} %constant.35.clone) | copy-start | bytes 7684
  196.1 24.0 %copy-start.2 = (f32[4,10]{1,0:T(4,128)S(1)}, f32[4,10]{1,0:T(4,128)}, u32[]{:S(2)}) copy-start(f32[4,10]{1,0:T(4,128)} %constant.40) | copy-start | bytes 484
where the time goes:
time: 222 us; the launch traced here: 221 us
  Pallas kernels  196 us (88%)
  local copies, waits for them, and re-layouts  16.5 us (7%)
  starting transfers between devices  4.38 us (2%)
    pallas_call x1, Pallas kernels, transformed(): pl.pallas_call(video_kernel, out_shape=(jax.ShapeDtypeStruct((frames, PER...  187 us
    transpose x1, local copies, waits for them, and re-layouts, shards(): coeffs = coeffs.transpose(0, 2, 1, 3).reshape(frames, rows, width)  11.7 us
    pallas_call x1, Pallas kernels, total_over_devices(): pl.pallas_call(total_kernel, out_shape=jax.ShapeDtypeStruct((8, 128), jnp...  9.8 us
  transfers between devices with their start and end apart: 2, of which 1 were waited for; matrix products, arithmetic and copies ran while one was open for 0% of the time, Pallas kernels for 0%

commit v1 on v0

v1 whole, which is shorter than its diff:
```python
import jax
import jax.numpy as jnp
import numpy as np
from jax import lax
from jax.experimental import pallas as pl
from jax.experimental.pallas import tpu as pltpu
from jax.sharding import PartitionSpec as P

SLEVELS = 3
TLEVELS = 3
PERIOD = 2**SLEVELS
MARGIN = 8
GROUP = 4
BLOCK = 256
LANES = 128

LIFT_ALPHA = -1.586134342
LIFT_BETA = -0.05298011854
LIFT_GAMMA = 0.8829110762
LIFT_DELTA = 0.4435068522
LIFT_ZETA = 1.149604398
STEPS = (LIFT_ALPHA, LIFT_BETA, LIFT_GAMMA, LIFT_DELTA)
MESH = pl.DeviceIdType.MESH


def level_of(number, ceiling):
    depth_now = 1
    while number % 2 == 0 and depth_now <= ceiling:
        number = number // 2
        depth_now = depth_now + 1
    return depth_now


def space_band(row_level, col_level, levels):
    finest = min(row_level, col_level)
    if finest > levels:
        return 3 * levels
    if row_level == col_level:
        return 3 * (finest - 1) + 2
    if row_level == finest:
        return 3 * (finest - 1)
    return 3 * (finest - 1) + 1


def lifted_identity(size):
    x = np.eye(size)
    after = np.concatenate([np.arange(2, size, 2), [size - 2]])
    before = np.concatenate([[1], np.arange(1, size - 1, 2)])
    even, odd = np.arange(0, size, 2), np.arange(1, size, 2)
    x[:, odd] += LIFT_ALPHA * (x[:, even] + x[:, after])
    x[:, even] += LIFT_BETA * (x[:, before] + x[:, odd])
    x[:, odd] += LIFT_GAMMA * (x[:, even] + x[:, after])
    x[:, even] += LIFT_DELTA * (x[:, before] + x[:, odd])
    x[:, even] *= LIFT_ZETA
    x[:, odd] *= 1.0 / LIFT_ZETA
    return x


def high_and_low(x):
    x = np.asarray(x, np.float32)
    high = x.astype(jnp.bfloat16)
    return np.stack([high, (x - high.astype(np.float32)).astype(jnp.bfloat16)])


def column_weights(width):
    tables = []
    for level in range(SLEVELS):
        s = 2**level
        matrix = np.eye(width)
        matrix[::s, ::s] = lifted_identity(width // s)
        middle = matrix[LANES : LANES + 2 * BLOCK, BLOCK : 2 * BLOCK]
        first = matrix[:LANES, :LANES]
        last = matrix[width - LANES :, width - LANES :]
        tables.append(high_and_low(np.concatenate([middle, np.hstack([first, last])])))
    return np.stack(tables)


def energy_tables(counted):
    lane = lax.broadcasted_iota(jnp.int32, (LANES, LANES), 0)
    column = lax.broadcasted_iota(jnp.int32, (LANES, LANES), 1)
    u = lane // (LANES // (SLEVELS + 1)) + 1
    v = jnp.full_like(lane, 1)
    for level in range(1, SLEVELS + 1):
        v = v + jnp.where(lane % 2**level == 0, 1, 0)
    finest = jnp.minimum(u, v)
    kind = jnp.where(u == v, 2, jnp.where(u == finest, 0, 1))
    band = jnp.where(finest > SLEVELS, 3 * SLEVELS, 3 * (finest - 1) + kind)
    member = jnp.where(band == column, (SLEVELS + 1) * PERIOD / LANES, 0.0)
    t = lax.broadcasted_iota(jnp.int32, (8, LANES), 0)
    s = lax.broadcasted_iota(jnp.int32, (8, LANES), 1)
    share = jnp.full((8, LANES), 1.0 / counted, jnp.float32)
    for i in range(TLEVELS + 1):
        share = jnp.where(t == i, share * float(2 ** min(i + 1, TLEVELS)), share)
    for i in range(3 * SLEVELS + 1):
        share = jnp.where(s == i, share * float(4 ** min(i // 3 + 1, SLEVELS)), share)
    return member, share


def outgoing(f):
    o = {i: f[i] if i % 4 == 1 else f[i] - 0.5 * (f[i - 1] + f[i + 1]) for i in range(1, 14, 2)}
    a = {i: f[i] + 0.25 * (o[i - 1] + o[i + 1]) for i in range(2, 13, 2)}
    p6 = a[6] - 0.5 * (a[4] + a[8])
    p10 = a[10] - 0.5 * (a[8] + a[12])
    b8 = a[8] + 0.25 * (p6 + p10)
    to_before = (f[0], o[1], a[2] - 0.5 * a[4])
    to_after = (
        f[15] - 0.5 * f[14],
        f[14] + 0.25 * o[13] - 0.5 * a[12],
        a[12] + 0.25 * p10 - 0.5 * b8,
    )
    return to_before, to_after


def temporal(f, before, after, is_first, is_last):
    o = {i: f[i] if i % 4 == 1 else f[i] - 0.5 * (f[i - 1] + f[i + 1]) for i in range(1, 14, 2)}
    f16 = jnp.where(is_last, f[14], after[0])
    o[15] = f[15] - 0.5 * (f[14] + f16)
    o[-1] = jnp.where(is_first, o[1], before[0] - 0.5 * f[0])
    a = {i: f[i] + 0.25 * (o[i - 1] + o[i + 1]) for i in range(0, 16, 2)}
    a16 = jnp.where(is_last, a[12], after[0] + 0.25 * (o[15] + after[1]))
    a[16] = a16
    p = {i: a[i] - 0.5 * (a[i - 2] + a[i + 2]) for i in range(2, 16, 4)}
    p[-2] = jnp.where(is_first, p[2], before[1] + 0.25 * o[-1] - 0.5 * a[0])
    b = {i: a[i] + 0.25 * (p[i - 2] + p[i + 2]) for i in range(0, 16, 4)}
    b[16] = jnp.where(is_last, b[8], a16 + 0.25 * (p[14] + after[2] - 0.5 * a16))
    d4 = b[4] - 0.5 * (b[0] + b[8])
    d12 = b[12] - 0.5 * (b[8] + b[16])
    dm4 = jnp.where(is_first, d4, before[2] + 0.25 * p[-2] - 0.5 * b[0])
    out = {i: o[i] for i in range(1, 16, 2)}
    out.update({i: p[i] for i in range(2, 16, 4)})
    out[4], out[12] = d4, d12
    out[0] = b[0] + 0.25 * (dm4 + d4)
    out[8] = b[8] + 0.25 * (d4 + d12)
    return out


def phase_at(q):
    half, quarter = q // 4, (q // 2) % 2
    return (
        (1 - half) * (2 * q + 1)
        + half * (1 - quarter) * (4 * (q % 2) + 2)
        + half * quarter * 4 * (q % 2)
    )


def video_kernel(x_ref, w_ref, result, energy,
                 planes, edges, high, low, buf, w_mid, w_first, w_last, held,
                 from_before, from_after, to_before, to_after, acc, packed, inbox,
                 x_sem, w_sem, e_send, e_recv, f_send, f_recv, f_own, h_send, h_recv,
                 r_send, r_recv, r_own, s_send, s_recv):
    frames, phases, inner, width = planes.shape
    groups = inner + 2 * MARGIN
    part = inner // GROUP
    kept = 1
    moved = [n for n in range(frames) if n != kept]
    me = lax.axis_index("frame")
    row = lax.axis_index("row")
    strips = lax.axis_size("row")
    count = lax.axis_size("frame")
    at_top = row == 0
    at_bottom = row == strips - 1
    member = me % GROUP
    base = me - member
    is_first = base == 0
    is_last = base == count - GROUP
    peers = [base + (member + k) % GROUP for k in range(1, GROUP)]

    all_devices = count * strips
    flat = me * strips + row

    def place(device):
        return {"frame": device // strips, "row": device % strips}

    barrier = pltpu.get_barrier_semaphore()

    def greet(j, carry):
        pl.semaphore_signal(
            barrier, inc=1, device_id=place((flat + j) % all_devices), device_id_type=MESH
        )
        return carry

    lax.fori_loop(1, all_devices, greet, 0)

    def weight_copies(level):
        sources = (
            (w_ref.at[level, :, 0 : 2 * BLOCK, :], w_mid.at[level]),
            (w_ref.at[level, :, 2 * BLOCK : 2 * BLOCK + LANES, 0:LANES],
             w_first.at[level, :, 0:LANES, 0:LANES]),
            (w_ref.at[level, :, LANES : 2 * LANES, LANES:BLOCK],
             w_first.at[level, :, 0:LANES, LANES:BLOCK]),
            (w_ref.at[level, :, 2 * LANES : 2 * BLOCK, :],
             w_first.at[level, :, LANES : LANES + BLOCK, :]),
            (w_ref.at[level, :, 2 * BLOCK : 2 * BLOCK + LANES, LANES:BLOCK],
             w_last.at[level, :, BLOCK : BLOCK + LANES, LANES:BLOCK]),
            (w_ref.at[level, :, BLOCK : BLOCK + LANES, 0:LANES],
             w_last.at[level, :, BLOCK : BLOCK + LANES, 0:LANES]),
            (w_ref.at[level, :, 0:BLOCK, :], w_last.at[level, :, 0:BLOCK, :]),
        )
        return [
            pltpu.make_async_copy(source, target, w_sem.at[level, i])
            for i, (source, target) in enumerate(sources)
        ]

    def fetch(n, p):
        return pltpu.make_async_copy(x_ref.at[n, :, p, :], planes.at[n, p], x_sem.at[n, p])

    def start_fetch(n):
        for p in range(phases):
            fetch(n, p).start()

    def edge(n, p, side):
        source = pl.ds(inner - MARGIN, MARGIN) if side == 0 else pl.ds(0, MARGIN)
        target = pl.ds(MARGIN, MARGIN) if side == 0 else pl.ds(0, MARGIN)
        return pltpu.make_async_remote_copy(
            src_ref=x_ref.at[n, source, p, :],
            dst_ref=edges.at[n, p, target, :],
            send_sem=e_send.at[side, n, p],
            recv_sem=e_recv.at[side, n, p],
            device_id={"row": row + 1 if side == 0 else row - 1},
            device_id_type=MESH,
        )

    for copy in weight_copies(0):
        copy.start()
    start_fetch(0)
    for level in range(1, SLEVELS):
        for copy in weight_copies(level):
            copy.start()
    for n in (2, 1, 3):
        start_fetch(n)

    pl.semaphore_wait(barrier, all_devices - 1)

    def every_edge(side, action):
        def one(n, carry):
            for p in range(phases):
                action(edge(n, p, side))
            return carry
        lax.fori_loop(0, frames, one, 0)

    @pl.when(jnp.logical_not(at_bottom))
    def _():
        every_edge(0, lambda copy: copy.start())

    @pl.when(jnp.logical_not(at_top))
    def _():
        every_edge(1, lambda copy: copy.start())

    def part_of(device):
        return pl.ds(pl.multiple_of((device % GROUP) * part, 8), part)

    def spot(device, n):
        return (device % GROUP) * frames + n

    def forward(n, c, k):
        peer = peers[k]
        return pltpu.make_async_remote_copy(
            src_ref=planes.at[n, c, part_of(peer), :],
            dst_ref=held.at[spot(me, n), c],
            send_sem=f_send.at[n, k, c],
            recv_sem=f_recv.at[n, k, c],
            device_id={"frame": peer},
            device_id_type=MESH,
        )

    def forward_own(n, c):
        return pltpu.make_async_copy(
            planes.at[n, c, part_of(me), :], held.at[spot(me, n), c], f_own.at[n, c]
        )

    def halo(c, side):
        return pltpu.make_async_remote_copy(
            src_ref=(to_before if side == 0 else to_after).at[c],
            dst_ref=(from_after if side == 0 else from_before).at[c],
            send_sem=h_send.at[side, c],
            recv_sem=h_recv.at[side, c],
            device_id={"frame": me - GROUP if side == 0 else me + GROUP},
            device_id_type=MESH,
        )

    def halo_sends(c, action):
        @pl.when(jnp.logical_not(is_first))
        def _():
            action(halo(c, 0))

        @pl.when(jnp.logical_not(is_last))
        def _():
            action(halo(c, 1))

    def halo_arrivals(c):
        @pl.when(jnp.logical_not(is_last))
        def _():
            halo(c, 0).wait_recv()

        @pl.when(jnp.logical_not(is_first))
        def _():
            halo(c, 1).wait_recv()

    def back(i, c, k):
        peer = peers[k]
        return pltpu.make_async_remote_copy(
            src_ref=held.at[spot(peer, moved[i]), c],
            dst_ref=result.at[moved[i], c, part_of(me), :],
            send_sem=r_send.at[i, k, c],
            recv_sem=r_recv.at[i, k, c],
            device_id={"frame": peer},
            device_id_type=MESH,
        )

    def back_own(i, c):
        return pltpu.make_async_copy(
            held.at[spot(me, moved[i]), c], result.at[moved[i], c, part_of(me), :], r_own.at[i, c]
        )

    def start_forward(n, c):
        for k in range(GROUP - 1):
            forward(n, c, k).start()
        forward_own(n, c).start()

    def split(rows, lanes, value):
        rounded = value.astype(jnp.bfloat16)
        high[rows, lanes] = rounded
        low[rows, lanes] = (value - rounded.astype(jnp.float32)).astype(jnp.bfloat16)

    everything = pl.ds(0, width)
    tile = 16

    def one_frame(step, carry):
        n = (2 * step) % 3 + 3 * (step // 3)
        for p in range(phases):
            fetch(n, p).wait()

        def take(p, carry):
            for r in range(0, inner, tile):
                rows = pl.ds(pl.multiple_of(p * groups + r, tile), tile)
                split(rows, everything, planes[n, p, pl.ds(r, tile), :])
            return carry

        lax.fori_loop(0, phases, take, 0)

        @pl.when(jnp.logical_not(at_top))
        def _():
            for p in range(phases):
                edge(n, p, 0).wait_recv()

        @pl.when(jnp.logical_not(at_bottom))
        def _():
            for p in range(phases):
                edge(n, p, 1).wait_recv()

        def take_edges(p, carry):
            rows = pl.ds(pl.multiple_of(p * groups + inner, tile), tile)
            split(rows, everything, edges[n, p])
            return carry

        lax.fori_loop(0, phases, take_edges, 0)

        for level in range(SLEVELS):
            s = 2**level
            height = groups * (phases // s)

            @pl.when(step == 0)
            def _(level=level):
                for copy in weight_copies(level):
                    copy.wait()

            for b in range(width // BLOCK):
                if b == 0:
                    w, start, depth = w_first, 0, BLOCK + LANES
                elif b == width // BLOCK - 1:
                    w, start, depth = w_last, width - BLOCK - LANES, BLOCK + LANES
                else:
                    w, start, depth = w_mid, b * BLOCK - LANES, 2 * BLOCK
                xh = high[0:height, start : start + depth]
                xl = low[0:height, start : start + depth]
                wh, wl = w[level, 0], w[level, 1]
                buf[0:height, b * BLOCK : (b + 1) * BLOCK] = jnp.dot(
                    jnp.concatenate([xh, xl, xh], axis=1),
                    jnp.concatenate([wh, wh, wl], axis=0),
                    preferred_element_type=jnp.float32,
                )

            def rows(i, carry, level=level, s=s):
                lanes = pl.ds(pl.multiple_of(i * LANES, LANES), LANES)
                lane = lax.broadcasted_iota(jnp.int32, (1, LANES), 1)
                on = lane % s == 0
                x = {
                    p: buf[pl.ds(groups * (p // s), groups), lanes] for p in range(0, phases, s)
                }
                index = lax.broadcasted_iota(jnp.int32, (groups, LANES), 0)
                first = jnp.logical_and(index == 0, at_top)
                last = jnp.logical_and(index == inner - 1, at_bottom)
                for number, factor in enumerate(STEPS):
                    c = jnp.where(on, factor, 0.0)
                    if number % 2 == 0:
                        for p in range(s, phases, 2 * s):
                            if p + s < phases:
                                after = x[p + s]
                            else:
                                after = jnp.where(last, x[p - s], pltpu.roll(x[0], groups - 1, 0))
                            x[p] = x[p] + c * (x[p - s] + after)
                    else:
                        for p in range(0, phases, 2 * s):
                            if p > 0:
                                before = x[p - s]
                            else:
                                before = jnp.where(first, x[s], pltpu.roll(x[phases - s], 1, 0))
                            x[p] = x[p] + c * (before + x[p + s])
                up = jnp.where(on, LIFT_ZETA, 1.0)
                down = jnp.where(on, 1.0 / LIFT_ZETA, 1.0)
                for p in x:
                    is_low = p % (2 * s) == 0
                    value = x[p] * (up if is_low else down)
                    if is_low and level < SLEVELS - 1:
                        split(pl.ds(groups * (p // (2 * s)), groups), lanes, value)
                    else:
                        planes[n, p, :, lanes] = value[:inner]
                return carry

            lax.fori_loop(0, width // LANES, rows, 0)

            done = [
                p for p in range(0, phases, s) if p % (2 * s) != 0 or level == SLEVELS - 1
            ]

            @pl.when(step != 2)
            def _(done=done):
                for c in done:
                    start_forward(n, c)

        @pl.when(step == 2)
        def _():
            def high_frame(q, carry):
                c = phase_at(q)
                high_part = planes[kept, c] - 0.5 * (planes[kept - 1, c] + planes[kept + 1, c])
                planes[kept, c] = high_part
                result[kept, c] = high_part
                start_forward(kept, c)
                return carry

            lax.fori_loop(0, phases, high_frame, 0)

        return carry

    lax.fori_loop(0, frames, one_frame, 0)
    total = GROUP * frames

    def send_halo(q):
        c = phase_at(q)
        for n in range(frames):
            for k in range(GROUP - 1):
                forward(n, c, k).wait_recv()
            forward_own(n, c).wait()

        def strip(i, carry):
            lanes = pl.ds(pl.multiple_of(i * LANES, LANES), LANES)
            left, right = outgoing([held[n, c, :, lanes] for n in range(total)])
            for j in range(TLEVELS):
                to_before[c, j, :, lanes] = left[j]
                to_after[c, j, :, lanes] = right[j]
            return carry

        lax.fori_loop(0, width // LANES, strip, 0)
        halo_sends(c, lambda copy: copy.start())

    def finish(q):
        c = phase_at(q)
        halo_arrivals(c)

        def strip(i, carry):
            lanes = pl.ds(pl.multiple_of(i * LANES, LANES), LANES)
            f = [held[n, c, :, lanes] for n in range(total)]
            before = [from_before[c, j, :, lanes] for j in range(TLEVELS)]
            after = [from_after[c, j, :, lanes] for j in range(TLEVELS)]
            out = temporal(f, before, after, is_first, is_last)
            sums = [None] * (TLEVELS + 1)
            for n in range(total):
                if n % frames in moved:
                    held[n, c, :, lanes] = out[n]
                t = level_of(n % 2**TLEVELS, TLEVELS) - 1
                square = out[n] * out[n]
                sums[t] = square if sums[t] is None else sums[t] + square
            return tuple(
                carry[t] + jnp.sum(sums[t].reshape(part // 8, 8, LANES), axis=0)
                for t in range(TLEVELS + 1)
            )

        zero = jnp.zeros((8, LANES), jnp.float32)
        sums = lax.fori_loop(0, width // LANES, strip, (zero,) * (TLEVELS + 1))
        for t in range(TLEVELS + 1):
            acc[c, t] = sums[t]
        for i in range(len(moved)):
            for k in range(GROUP - 1):
                back(i, c, k).start()
            back_own(i, c).start()

    send_halo(0)

    def middle(q, carry):
        send_halo(q)
        finish(q - 1)
        return carry

    lax.fori_loop(1, phases, middle, 0)
    finish(phases - 1)

    lane = lax.broadcasted_iota(jnp.int32, (1, LANES), 1)
    packed[...] = jnp.zeros_like(packed)
    for t in range(TLEVELS + 1):
        line = jnp.zeros((1, LANES), jnp.float32)
        for u in range(1, SLEVELS + 2):
            mine = sum(acc[c, t] for c in range(phases) if level_of(c, SLEVELS) == u)
            mine = jnp.sum(mine, axis=0, keepdims=True)
            distance = PERIOD
            while distance < LANES:
                mine = mine + pltpu.roll(mine, distance, 1)
                distance = 2 * distance
            line = jnp.where(lane // (LANES // (SLEVELS + 1)) == u - 1, mine, line)
        packed[pl.ds(t, 1), :] = line

    def to_other(j):
        return pltpu.make_async_remote_copy(
            src_ref=packed,
            dst_ref=inbox.at[flat],
            send_sem=s_send.at[j],
            recv_sem=s_recv.at[flat],
            device_id=place((flat + j) % all_devices),
            device_id_type=MESH,
        )

    def start_sums(j, carry):
        to_other(j).start()
        return carry

    lax.fori_loop(1, all_devices, start_sums, 0)
    inbox[flat] = packed[...]

    def arrive(j, carry):
        source = (flat + j) % all_devices
        pltpu.make_async_remote_copy(
            src_ref=packed,
            dst_ref=inbox.at[source],
            send_sem=s_send.at[j],
            recv_sem=s_recv.at[source],
            device_id=place(source),
            device_id_type=MESH,
        ).wait_recv()
        return carry

    lax.fori_loop(1, all_devices, arrive, 0)
    sums = lax.fori_loop(1, all_devices, lambda j, s: s + inbox[j], inbox[0])
    counted = float(count * frames * strips * inner * phases * width)
    band, share = energy_tables(counted)
    energy[...] = share * jnp.dot(
        sums, band, precision=lax.Precision.HIGHEST, preferred_element_type=jnp.float32
    )

    def drain(c, carry):
        for k in range(GROUP - 1):
            for n in range(frames):
                forward(n, c, k).wait_send()
            for i in range(len(moved)):
                back(i, c, k).wait()
        halo_sends(c, lambda copy: copy.wait_send())
        for i in range(len(moved)):
            back_own(i, c).wait()
        return carry

    lax.fori_loop(0, phases, drain, 0)

    @pl.when(jnp.logical_not(at_bottom))
    def _():
        every_edge(0, lambda copy: copy.wait_send())

    @pl.when(jnp.logical_not(at_top))
    def _():
        every_edge(1, lambda copy: copy.wait_send())

    def drain_sums(j, carry):
        to_other(j).wait_send()
        return carry

    lax.fori_loop(1, all_devices, drain_sums, 0)


def weave_kernel(planes, energy, o_ref, e_ref, sem):
    frames, phases = planes.shape[:2]
    copies = [
        pltpu.make_async_copy(planes.at[n, p], o_ref.at[n, :, p, :], sem.at[n, p])
        for n in range(frames)
        for p in range(phases)
    ]
    for copy in copies:
        copy.start()
    e_ref[...] = energy[: TLEVELS + 1, : 3 * SLEVELS + 1]
    for copy in copies:
        copy.wait()


def shards(footage):
    frames, rows, width = footage.shape
    inner = rows // PERIOD
    groups = inner + 2 * MARGIN
    part = inner // GROUP
    strips = lax.axis_size("row")
    devices = lax.axis_size("frame") * strips
    any_space = pl.BlockSpec(memory_space=pl.ANY)
    vmem = pl.BlockSpec(memory_space=pltpu.VMEM)
    f32, bf16 = jnp.float32, jnp.bfloat16
    halo_buffer = pltpu.VMEM((PERIOD, TLEVELS, part, width), f32)
    dma = pltpu.SemaphoreType.DMA
    sent = frames - 1
    planes, energy = pl.pallas_call(
        video_kernel,
        out_shape=(
            jax.ShapeDtypeStruct((frames, PERIOD, inner, width), f32),
            jax.ShapeDtypeStruct((8, LANES), f32),
        ),
        in_specs=[any_space, pl.BlockSpec(memory_space=pltpu.HBM)],
        out_specs=(vmem, vmem),
        scratch_shapes=[
            pltpu.VMEM((frames, PERIOD, inner, width), f32),
            pltpu.VMEM((frames, PERIOD, 2 * MARGIN, width), f32),
            pltpu.VMEM((PERIOD * groups, width), bf16),
            pltpu.VMEM((PERIOD * groups, width), bf16),
            pltpu.VMEM((PERIOD * groups, width), f32),
            pltpu.VMEM((SLEVELS, 2, 2 * BLOCK, BLOCK), bf16),
            pltpu.VMEM((SLEVELS, 2, BLOCK + LANES, BLOCK), bf16),
            pltpu.VMEM((SLEVELS, 2, BLOCK + LANES, BLOCK), bf16),
            pltpu.VMEM((GROUP * frames, PERIOD, part, width), f32),
            halo_buffer, halo_buffer, halo_buffer, halo_buffer,
            pltpu.VMEM((PERIOD, TLEVELS + 1, 8, LANES), f32),
            pltpu.VMEM((8, LANES), f32),
            pltpu.VMEM((devices, 8, LANES), f32),
            dma((frames, PERIOD)), dma((SLEVELS, 7)),
            dma((2, frames, PERIOD)), dma((2, frames, PERIOD)),
            dma((frames, GROUP - 1, PERIOD)), dma((frames, GROUP - 1, PERIOD)),
            dma((frames, PERIOD)),
            dma((2, PERIOD)), dma((2, PERIOD)),
            dma((sent, GROUP - 1, PERIOD)), dma((sent, GROUP - 1, PERIOD)),
            dma((sent, PERIOD)),
            dma((devices,)), dma((devices,)),
        ],
        compiler_params=pltpu.CompilerParams(
            collective_id=0, has_side_effects=True, vmem_limit_bytes=40 * 2**20
        ),
    )(
        footage.reshape(frames, inner, PERIOD, width),
        jnp.asarray(column_weights(width)),
    )
    coeffs, means = pl.pallas_call(
        weave_kernel,
        out_shape=(
            jax.ShapeDtypeStruct((frames, inner, PERIOD, width), f32),
            jax.ShapeDtypeStruct((TLEVELS + 1, 3 * SLEVELS + 1), f32),
        ),
        in_specs=[vmem, vmem],
        out_specs=(any_space, vmem),
        scratch_shapes=[dma((frames, PERIOD))],
        compiler_params=pltpu.CompilerParams(vmem_limit_bytes=20 * 2**20),
    )(planes, energy)
    return coeffs.reshape(frames, rows, width), means


def solution(mesh):
    return jax.shard_map(
        shards,
        mesh=mesh,
        in_specs=(P("frame", "row", None),),
        out_specs=(P("frame", "row", None), P()),
        check_vma=False,
    )
```

time: 222 us -> 186 us (0.84)
  local copies, waits for them, and re-layouts: 16.5 us -> 1.54 us
  Pallas kernels: 196 us -> 183 us
  starting transfers between devices: 4.38 us -> 0 us
    pallas_call x2, Pallas kernels: 196 us -> 183 us  [the longest x1 179 us: shards(): pl.pallas_call(video_kernel, out_shape=(jax.ShapeDtypeStruct((frames, PER...]
    transpose x1 -> x0, local copies, waits for them, and re-layouts: 11.7 us -> none  [shards(): coeffs = coeffs.transpose(0, 2, 1, 3).reshape(frames, rows, width)]
    ppermute x2 -> x0, starting transfers between devices: 4.38 us -> none  [shifted(): return lax.ppermute(block, axis, route)]
    reshape x3 -> x0, local copies, waits for them, and re-layouts: 2.8 us -> none  [the longest x1 1.59 us: transformed(): halo = halo.reshape(frames, 2 * MARGIN, PERIOD, width).transpose(0, 2, 1, 3)]
  transfers between devices with their start and end apart: 2 -> 0, of which waited for: 1 -> 0; matrix products, arithmetic and copies ran while one was open for 0% -> 0% of each run, Pallas kernels for 0% -> 0%
where the time goes in v1:
time: 186 us
  Pallas kernels  183 us (98%)
    pallas_call x1, Pallas kernels, shards(): pl.pallas_call(video_kernel, out_shape=(jax.ShapeDtypeStruct((frames, PER...  179 us
    pallas_call x1, Pallas kernels, shards(): pl.pallas_call(weave_kernel, out_shape=(jax.ShapeDtypeStruct((frames, inn...  4.12 us

profile of v1, /device:TPU:0, one launch (start us, length us, event | category | flops | bytes accessed | tf_op | source)
XLA Modules:
  0.0 185.7 jit_solution(10878877888696810768)
XLA Ops:
  0.6 0.0 copy-start
  0.6 1.5 copy-done
  2.2 179.4 %shard_map.41 = (f32[4,8,64,1024]{3,2,1,0:T(8,128)S(1)}, f32[8,128]{1,0:T(8,128)S(1)}) custom-call(f32[4,64,8,1024]{3,2,1,0:T(8,128)} %bitcast.2, bf16[3,2,640,256]{3,2,1,0:T(8,128)(2,1)S(1)} %copy-done), custom_call_target="tpu_custom_call" | custom-call | tf_op jit(solution)/shard_map/pallas_call | solution.py:613
  181.6 4.1 %shard_map.42 = (f32[4,64,8,1024]{3,2,1,0:T(8,128)}, f32[4,10]{1,0:T(4,128)}) custom-call(f32[4,8,64,1024]{3,2,1,0:T(8,128)S(1)} %get-tuple-element.6.planes, f32[8,128]{1,0:T(8,128)S(1)} %get-tuple-element.7.energy), custom_call_target="tpu_custom_call" | custom-call | tf_op jit(solution)/shard_map/pallas_call | solution.py:651
Async XLA Ops:
  0.6 1.5 copy-start

commit v2 on v1

--- a/solution.py
+++ b/solution.py
@@ -181,6 +181,9 @@
 
     lax.fori_loop(1, all_devices, greet, 0)
 
+    def arrived(ref, sem):
+        pltpu.make_async_copy(ref, ref, sem).wait()
+
     def weight_copies(level):
         sources = (
             (w_ref.at[level, :, 0 : 2 * BLOCK, :], w_mid.at[level]),
@@ -197,12 +200,16 @@
             (w_ref.at[level, :, 0:BLOCK, :], w_last.at[level, :, 0:BLOCK, :]),
         )
         return [
-            pltpu.make_async_copy(source, target, w_sem.at[level, i])
-            for i, (source, target) in enumerate(sources)
+            pltpu.make_async_copy(source, target, w_sem.at[level, kind])
+            for (source, target), kind in zip(sources, (0, 1, 1, 1, 2, 2, 2))
         ]
 
+    def await_weights(level):
+        for kind, w in enumerate((w_mid, w_first, w_last)):
+            arrived(w.at[level], w_sem.at[level, kind])
+
     def fetch(n, p):
-        return pltpu.make_async_copy(x_ref.at[n, :, p, :], planes.at[n, p], x_sem.at[n, p])
+        return pltpu.make_async_copy(x_ref.at[n, :, p, :], planes.at[n, p], x_sem.at[n])
 
     def start_fetch(n):
         for p in range(phases):
@@ -214,8 +221,8 @@
         return pltpu.make_async_remote_copy(
             src_ref=x_ref.at[n, source, p, :],
             dst_ref=edges.at[n, p, target, :],
-            send_sem=e_send.at[side, n, p],
-            recv_sem=e_recv.at[side, n, p],
+            send_sem=e_send.at[side],
+            recv_sem=e_recv.at[side, n],
             device_id={"row": row + 1 if side == 0 else row - 1},
             device_id_type=MESH,
         )
@@ -231,20 +238,20 @@
 
     pl.semaphore_wait(barrier, all_devices - 1)
 
-    def every_edge(side, action):
+    def start_edges(side):
         def one(n, carry):
             for p in range(phases):
-                action(edge(n, p, side))
+                edge(n, p, side).start()
             return carry
         lax.fori_loop(0, frames, one, 0)
 
     @pl.when(jnp.logical_not(at_bottom))
     def _():
-        every_edge(0, lambda copy: copy.start())
+        start_edges(0)
 
     @pl.when(jnp.logical_not(at_top))
     def _():
-        every_edge(1, lambda copy: copy.start())
+        start_edges(1)
 
     def part_of(device):
         return pl.ds(pl.multiple_of((device % GROUP) * part, 8), part)
@@ -257,35 +264,35 @@
         return pltpu.make_async_remote_copy(
             src_ref=planes.at[n, c, part_of(peer), :],
             dst_ref=held.at[spot(me, n), c],
-            send_sem=f_send.at[n, k, c],
-            recv_sem=f_recv.at[n, k, c],
+            send_sem=f_send.at[k],
+            recv_sem=f_recv.at[c],
             device_id={"frame": peer},
             device_id_type=MESH,
         )
 
     def forward_own(n, c):
         return pltpu.make_async_copy(
-            planes.at[n, c, part_of(me), :], held.at[spot(me, n), c], f_own.at[n, c]
+            planes.at[n, c, part_of(me), :], held.at[spot(me, n), c], f_own.at[c]
         )
 
     def halo(c, side):
         return pltpu.make_async_remote_copy(
             src_ref=(to_before if side == 0 else to_after).at[c],
             dst_ref=(from_after if side == 0 else from_before).at[c],
-            send_sem=h_send.at[side, c],
+            send_sem=h_send.at[side],
             recv_sem=h_recv.at[side, c],
             device_id={"frame": me - GROUP if side == 0 else me + GROUP},
             device_id_type=MESH,
         )
 
-    def halo_sends(c, action):
+    def start_halos(c):
         @pl.when(jnp.logical_not(is_first))
         def _():
-            action(halo(c, 0))
+            halo(c, 0).start()
 
         @pl.when(jnp.logical_not(is_last))
         def _():
-            action(halo(c, 1))
+            halo(c, 1).start()
 
     def halo_arrivals(c):
         @pl.when(jnp.logical_not(is_last))
@@ -301,15 +308,15 @@
         return pltpu.make_async_remote_copy(
             src_ref=held.at[spot(peer, moved[i]), c],
             dst_ref=result.at[moved[i], c, part_of(me), :],
-            send_sem=r_send.at[i, k, c],
-            recv_sem=r_recv.at[i, k, c],
+            send_sem=r_send.at[k],
+            recv_sem=r_recv.at[k],
             device_id={"frame": peer},
             device_id_type=MESH,
         )
 
     def back_own(i, c):
         return pltpu.make_async_copy(
-            held.at[spot(me, moved[i]), c], result.at[moved[i], c, part_of(me), :], r_own.at[i, c]
+            held.at[spot(me, moved[i]), c], result.at[moved[i], c, part_of(me), :], r_own
         )
 
     def start_forward(n, c):
@@ -327,8 +334,7 @@
 
     def one_frame(step, carry):
         n = (2 * step) % 3 + 3 * (step // 3)
-        for p in range(phases):
-            fetch(n, p).wait()
+        arrived(planes.at[n], x_sem.at[n])
 
         def take(p, carry):
             for r in range(0, inner, tile):
@@ -340,13 +346,11 @@
 
         @pl.when(jnp.logical_not(at_top))
         def _():
-            for p in range(phases):
-                edge(n, p, 0).wait_recv()
+            arrived(edges.at[n, :, pl.ds(MARGIN, MARGIN), :], e_recv.at[0, n])
 
         @pl.when(jnp.logical_not(at_bottom))
         def _():
-            for p in range(phases):
-                edge(n, p, 1).wait_recv()
+            arrived(edges.at[n, :, pl.ds(0, MARGIN), :], e_recv.at[1, n])
 
         def take_edges(p, carry):
             rows = pl.ds(pl.multiple_of(p * groups + inner, tile), tile)
@@ -361,8 +365,7 @@
 
             @pl.when(step == 0)
             def _(level=level):
-                for copy in weight_copies(level):
-                    copy.wait()
+                await_weights(level)
 
             for b in range(width // BLOCK):
                 if b == 0:
@@ -447,10 +450,8 @@
 
     def send_halo(q):
         c = phase_at(q)
-        for n in range(frames):
-            for k in range(GROUP - 1):
-                forward(n, c, k).wait_recv()
-            forward_own(n, c).wait()
+        arrived(held.at[pl.ds(0, total - frames), c], f_recv.at[c])
+        arrived(held.at[pl.ds(0, frames), c], f_own.at[c])
 
         def strip(i, carry):
             lanes = pl.ds(pl.multiple_of(i * LANES, LANES), LANES)
@@ -461,7 +462,7 @@
             return carry
 
         lax.fori_loop(0, width // LANES, strip, 0)
-        halo_sends(c, lambda copy: copy.start())
+        start_halos(c)
 
     def finish(q):
         c = phase_at(q)
@@ -522,8 +523,8 @@
         return pltpu.make_async_remote_copy(
             src_ref=packed,
             dst_ref=inbox.at[flat],
-            send_sem=s_send.at[j],
-            recv_sem=s_recv.at[flat],
+            send_sem=s_send,
+            recv_sem=s_recv,
             device_id=place((flat + j) % all_devices),
             device_id_type=MESH,
         )
@@ -535,19 +536,7 @@
     lax.fori_loop(1, all_devices, start_sums, 0)
     inbox[flat] = packed[...]
 
-    def arrive(j, carry):
-        source = (flat + j) % all_devices
-        pltpu.make_async_remote_copy(
-            src_ref=packed,
-            dst_ref=inbox.at[source],
-            send_sem=s_send.at[j],
-            recv_sem=s_recv.at[source],
-            device_id=place(source),
-            device_id_type=MESH,
-        ).wait_recv()
-        return carry
-
-    lax.fori_loop(1, all_devices, arrive, 0)
+    arrived(inbox.at[pl.ds(0, all_devices - 1)], s_recv)
     sums = lax.fori_loop(1, all_devices, lambda j, s: s + inbox[j], inbox[0])
     counted = float(count * frames * strips * inner * phases * width)
     band, share = energy_tables(counted)
@@ -555,46 +544,37 @@
         sums, band, precision=lax.Precision.HIGHEST, preferred_element_type=jnp.float32
     )
 
-    def drain(c, carry):
-        for k in range(GROUP - 1):
-            for n in range(frames):
-                forward(n, c, k).wait_send()
-            for i in range(len(moved)):
-                back(i, c, k).wait()
-        halo_sends(c, lambda copy: copy.wait_send())
-        for i in range(len(moved)):
-            back_own(i, c).wait()
-        return carry
-
-    lax.fori_loop(0, phases, drain, 0)
+    for k in range(GROUP - 1):
+        arrived(held.at[pl.ds(0, frames)], f_send.at[k])
+        arrived(held.at[pl.ds(0, len(moved))], r_send.at[k])
+        arrived(held.at[pl.ds(0, len(moved))], r_recv.at[k])
+    arrived(held.at[pl.ds(0, len(moved))], r_own)
+    arrived(inbox.at[pl.ds(0, all_devices - 1)], s_send)
+
+    @pl.when(jnp.logical_not(is_first))
+    def _():
+        arrived(to_before, h_send.at[0])
+
+    @pl.when(jnp.logical_not(is_last))
+    def _():
+        arrived(to_after, h_send.at[1])
 
     @pl.when(jnp.logical_not(at_bottom))
     def _():
-        every_edge(0, lambda copy: copy.wait_send())
+        arrived(edges.at[:, :, pl.ds(MARGIN, MARGIN), :], e_send.at[0])
 
     @pl.when(jnp.logical_not(at_top))
     def _():
-        every_edge(1, lambda copy: copy.wait_send())
-
-    def drain_sums(j, carry):
-        to_other(j).wait_send()
-        return carry
-
-    lax.fori_loop(1, all_devices, drain_sums, 0)
+        arrived(edges.at[:, :, pl.ds(0, MARGIN), :], e_send.at[1])
 
 
 def weave_kernel(planes, energy, o_ref, e_ref, sem):
     frames, phases = planes.shape[:2]
-    copies = [
-        pltpu.make_async_copy(planes.at[n, p], o_ref.at[n, :, p, :], sem.at[n, p])
-        for n in range(frames)
-        for p in range(phases)
-    ]
-    for copy in copies:
-        copy.start()
+    for n in range(frames):
+        for p in range(phases):
+            pltpu.make_async_copy(planes.at[n, p], o_ref.at[n, :, p, :], sem).start()
     e_ref[...] = energy[: TLEVELS + 1, : 3 * SLEVELS + 1]
-    for copy in copies:
-        copy.wait()
+    pltpu.make_async_copy(planes, planes, sem).wait()
 
 
 def shards(footage):
@@ -609,7 +589,6 @@
     f32, bf16 = jnp.float32, jnp.bfloat16
     halo_buffer = pltpu.VMEM((PERIOD, TLEVELS, part, width), f32)
     dma = pltpu.SemaphoreType.DMA
-    sent = frames - 1
     planes, energy = pl.pallas_call(
         video_kernel,
         out_shape=(
@@ -632,14 +611,12 @@
             pltpu.VMEM((PERIOD, TLEVELS + 1, 8, LANES), f32),
             pltpu.VMEM((8, LANES), f32),
             pltpu.VMEM((devices, 8, LANES), f32),
-            dma((frames, PERIOD)), dma((SLEVELS, 7)),
-            dma((2, frames, PERIOD)), dma((2, frames, PERIOD)),
-            dma((frames, GROUP - 1, PERIOD)), dma((frames, GROUP - 1, PERIOD)),
-            dma((frames, PERIOD)),
-            dma((2, PERIOD)), dma((2, PERIOD)),
-            dma((sent, GROUP - 1, PERIOD)), dma((sent, GROUP - 1, PERIOD)),
-            dma((sent, PERIOD)),
-            dma((devices,)), dma((devices,)),
+            dma((frames,)), dma((SLEVELS, 3)),
+            dma((2,)), dma((2, frames)),
+            dma((GROUP - 1,)), dma((PERIOD,)), dma((PERIOD,)),
+            dma((2,)), dma((2, PERIOD)),
+            dma((GROUP - 1,)), dma((GROUP - 1,)), dma,
+            dma, dma,
         ],
         compiler_params=pltpu.CompilerParams(
             collective_id=0, has_side_effects=True, vmem_limit_bytes=40 * 2**20
@@ -656,7 +633,7 @@
         ),
         in_specs=[vmem, vmem],
         out_specs=(any_space, vmem),
-        scratch_shapes=[dma((frames, PERIOD))],
+        scratch_shapes=[dma],
         compiler_params=pltpu.CompilerParams(vmem_limit_bytes=20 * 2**20),
     )(planes, energy)
     return coeffs.reshape(frames, rows, width), means

time: 186 us -> 179 us (0.962)
  Pallas kernels: 183 us -> 177 us
    pallas_call x1, Pallas kernels: 179 us -> 173 us  [shards(): pl.pallas_call(video_kernel, out_shape=(jax.ShapeDtypeStruct((frames, PER...]
where the time goes in v2:
time: 179 us
  Pallas kernels  177 us (99%)
    pallas_call x1, Pallas kernels, shards(): pl.pallas_call(video_kernel, out_shape=(jax.ShapeDtypeStruct((frames, PER...  173 us
    pallas_call x1, Pallas kernels, shards(): pl.pallas_call(weave_kernel, out_shape=(jax.ShapeDtypeStruct((frames, inn...  3.84 us

profile of v2, /device:TPU:0, one launch (start us, length us, event | category | flops | bytes accessed | tf_op | source)
XLA Modules:
  0.0 179.0 jit_solution(10224589362480430054)
XLA Ops:
  0.6 0.0 copy-start
  0.6 1.5 copy-done
  2.2 173.0 %shard_map.41 = (f32[4,8,64,1024]{3,2,1,0:T(8,128)S(1)}, f32[8,128]{1,0:T(8,128)S(1)}) custom-call(f32[4,64,8,1024]{3,2,1,0:T(8,128)} %bitcast.2, bf16[3,2,640,256]{3,2,1,0:T(8,128)(2,1)S(1)} %copy-done), custom_call_target="tpu_custom_call" | custom-call | tf_op jit(solution)/shard_map/pallas_call | solution.py:592
  175.2 3.8 %shard_map.42 = (f32[4,64,8,1024]{3,2,1,0:T(8,128)}, f32[4,10]{1,0:T(4,128)}) custom-call(f32[4,8,64,1024]{3,2,1,0:T(8,128)S(1)} %get-tuple-element.6.planes, f32[8,128]{1,0:T(8,128)S(1)} %get-tuple-element.7.energy), custom_call_target="tpu_custom_call" | custom-call | tf_op jit(solution)/shard_map/pallas_call | solution.py:628
Async XLA Ops:
  0.6 1.5 copy-start

commit v3 on v2

--- a/solution.py
+++ b/solution.py
@@ -11,6 +11,9 @@
 PERIOD = 2**SLEVELS
 MARGIN = 8
 GROUP = 4
+PAIRED = 6
+CUTS = 4
+DIRECT = 1
 BLOCK = 256
 LANES = 128
 
@@ -144,13 +147,18 @@
 
 
 def video_kernel(x_ref, w_ref, result, energy,
-                 planes, edges, high, low, buf, w_mid, w_first, w_last, held,
-                 from_before, from_after, to_before, to_after, acc, packed, inbox,
-                 x_sem, w_sem, e_send, e_recv, f_send, f_recv, f_own, h_send, h_recv,
-                 r_send, r_recv, r_own, s_send, s_recv):
+                 planes, edges, high, low, buf, w_mid, w_first, w_last,
+                 near_in, far_in, made, held, from_before, from_after, to_before, to_after,
+                 acc, packed, inbox, x_sem, w_sem, e_send, e_recv,
+                 n_send, n_recv, p_send, p_recv, d_send,
+                 f_send, f_recv, f_own, h_send, h_recv, r_send, r_recv, r_own, s_send, s_recv):
     frames, phases, inner, width = planes.shape
     groups = inner + 2 * MARGIN
     part = inner // GROUP
+    cut = inner // CUTS
+    chunks = PAIRED * CUTS
+    straight = DIRECT * CUTS
+    grouped = phases - PAIRED
     kept = 1
     moved = [n for n in range(frames) if n != kept]
     me = lax.axis_index("frame")
@@ -159,11 +167,18 @@
     count = lax.axis_size("frame")
     at_top = row == 0
     at_bottom = row == strips - 1
+    side = me % 2
+    is_left = side == 0
+    is_right = side == 1
+    is_first = me // 2 == 0
+    is_last = me // 2 == count // 2 - 1
     member = me % GROUP
     base = me - member
-    is_first = base == 0
-    is_last = base == count - GROUP
+    starts = base == 0
+    ends = base == count - GROUP
     peers = [base + (member + k) % GROUP for k in range(1, GROUP)]
+    partner = me + 1 - 2 * side
+    beyond = me - 2 + 4 * side
 
     all_devices = count * strips
     flat = me * strips + row
@@ -233,7 +248,7 @@
     for level in range(1, SLEVELS):
         for copy in weight_copies(level):
             copy.start()
-    for n in (2, 1, 3):
+    for n in (2, 3, 1):
         start_fetch(n)
 
     pl.semaphore_wait(barrier, all_devices - 1)
@@ -253,26 +268,95 @@
     def _():
         start_edges(1)
 
+    def both(a, b):
+        return jnp.logical_and(a, b)
+
+    def no(a):
+        return jnp.logical_not(a)
+
+    def rows_of(i):
+        return pl.ds(pl.multiple_of((i % CUTS) * cut, 8), cut)
+
+    def spot(i):
+        return phase_at(i // CUTS), rows_of(i)
+
+    def slot(i):
+        return i // CUTS, rows_of(i)
+
+    def near(kind, i, source):
+        return pltpu.make_async_remote_copy(
+            src_ref=source,
+            dst_ref=near_in.at[(kind,) + slot(i)],
+            send_sem=n_send.at[kind],
+            recv_sem=n_recv.at[kind, i],
+            device_id={"frame": partner},
+            device_id_type=MESH,
+        )
+
+    def far(kind, i, source):
+        return pltpu.make_async_remote_copy(
+            src_ref=source,
+            dst_ref=far_in.at[(kind,) + slot(i)],
+            send_sem=p_send.at[kind],
+            recv_sem=p_recv.at[kind, i],
+            device_id={"frame": beyond},
+            device_id_type=MESH,
+        )
+
+    def direct(i, source):
+        return pltpu.make_async_remote_copy(
+            src_ref=source,
+            dst_ref=near_in.at[(0,) + slot(i)],
+            send_sem=d_send,
+            recv_sem=n_recv.at[0, i],
+            device_id={"frame": me - 1},
+            device_id_type=MESH,
+        )
+
+    def take_near(kind, i):
+        at = (kind,) + slot(i)
+        arrived(near_in.at[at], n_recv.at[kind, i])
+        return near_in[at]
+
+    def await_far(kind, i):
+        arrived(far_in.at[(kind,) + slot(i)], p_recv.at[kind, i])
+
+    def take_far(kind, i):
+        await_far(kind, i)
+        return far_in[(kind,) + slot(i)]
+
+    def relay(i, carry):
+        await_far(0, i)
+        near(0, i, far_in.at[(0,) + slot(i)]).start()
+        return carry
+
+    def relay_some(start, stop):
+        @pl.when(both(is_left, no(is_last)))
+        def _():
+            lax.fori_loop(start, stop, relay, 0)
+
     def part_of(device):
         return pl.ds(pl.multiple_of((device % GROUP) * part, 8), part)
 
-    def spot(device, n):
+    def seat(device, n):
         return (device % GROUP) * frames + n
 
-    def forward(n, c, k):
+    def forward(n, g, k):
         peer = peers[k]
         return pltpu.make_async_remote_copy(
-            src_ref=planes.at[n, c, part_of(peer), :],
-            dst_ref=held.at[spot(me, n), c],
+            src_ref=planes.at[n, phase_at(PAIRED + g), part_of(peer), :],
+            dst_ref=held.at[seat(me, n), g],
             send_sem=f_send.at[k],
-            recv_sem=f_recv.at[c],
+            recv_sem=f_recv.at[g],
             device_id={"frame": peer},
             device_id_type=MESH,
         )
 
-    def forward_own(n, c):
+    def forward_own(n, g):
         return pltpu.make_async_copy(
-            planes.at[n, c, part_of(me), :], held.at[spot(me, n), c], f_own.at[c]
+            planes.at[n, phase_at(PAIRED + g), part_of(me), :],
+            held.at[seat(me, n), g],
+            f_own.at[g],
         )
 
     def halo(c, side):
@@ -286,28 +370,28 @@
         )
 
     def start_halos(c):
-        @pl.when(jnp.logical_not(is_first))
+        @pl.when(jnp.logical_not(starts))
         def _():
             halo(c, 0).start()
 
-        @pl.when(jnp.logical_not(is_last))
+        @pl.when(jnp.logical_not(ends))
         def _():
             halo(c, 1).start()
 
     def halo_arrivals(c):
-        @pl.when(jnp.logical_not(is_last))
+        @pl.when(jnp.logical_not(ends))
         def _():
             halo(c, 0).wait_recv()
 
-        @pl.when(jnp.logical_not(is_first))
+        @pl.when(jnp.logical_not(starts))
         def _():
             halo(c, 1).wait_recv()
 
     def back(i, c, k):
         peer = peers[k]
         return pltpu.make_async_remote_copy(
-            src_ref=held.at[spot(peer, moved[i]), c],
-            dst_ref=result.at[moved[i], c, part_of(me), :],
+            src_ref=held.at[seat(peer, moved[i]), c],
+            dst_ref=result.at[moved[i], phase_at(PAIRED + c), part_of(me), :],
             send_sem=r_send.at[k],
             recv_sem=r_recv.at[k],
             device_id={"frame": peer},
@@ -316,7 +400,9 @@
 
     def back_own(i, c):
         return pltpu.make_async_copy(
-            held.at[spot(me, moved[i]), c], result.at[moved[i], c, part_of(me), :], r_own
+            held.at[seat(me, moved[i]), c],
+            result.at[moved[i], phase_at(PAIRED + c), part_of(me), :],
+            r_own,
         )
 
     def start_forward(n, c):
@@ -333,7 +419,7 @@
     tile = 16
 
     def one_frame(step, carry):
-        n = (2 * step) % 3 + 3 * (step // 3)
+        n = (2 * step) % 5 - (step // 2) * (1 - step % 2)
         arrived(planes.at[n], x_sem.at[n])
 
         def take(p, carry):
@@ -426,30 +512,92 @@
                 p for p in range(0, phases, s) if p % (2 * s) != 0 or level == SLEVELS - 1
             ]
 
-            @pl.when(step != 2)
+            order = [phase_at(q) for q in range(phases)]
+
+            def first_frames(to_right, done=done):
+                for c in done:
+                    if order.index(c) < PAIRED:
+                        for r in range(CUTS):
+                            i = order.index(c) * CUTS + r
+                            source = planes.at[(0,) + spot(i)]
+                            if to_right:
+                                near(0, i, source).start()
+                            elif i < straight:
+                                direct(i, source).start()
+                            else:
+                                far(0, i, source).start()
+
+            @pl.when(both(step == 0, is_right))
+            def _(first_frames=first_frames):
+                first_frames(True)
+
+            @pl.when(both(step == 0, both(is_left, no(is_first))))
+            def _(first_frames=first_frames):
+                first_frames(False)
+
+            @pl.when(step != 3)
             def _(done=done):
                 for c in done:
-                    start_forward(n, c)
+                    if order.index(c) >= PAIRED:
+                        start_forward(n, order.index(c) - PAIRED)
 
         @pl.when(step == 2)
         def _():
-            def high_frame(q, carry):
-                c = phase_at(q)
-                high_part = planes[kept, c] - 0.5 * (planes[kept - 1, c] + planes[kept + 1, c])
-                planes[kept, c] = high_part
-                result[kept, c] = high_part
-                start_forward(kept, c)
+            def last_frame(i, carry):
+                at = (3,) + spot(i)
+                planes[at] = planes[at] - 0.5 * planes[(2,) + spot(i)]
+
+                @pl.when(both(is_right, no(is_last)))
+                def _():
+                    far(0, i, planes.at[(3,) + spot(i)]).start()
+
                 return carry
 
-            lax.fori_loop(0, phases, high_frame, 0)
+            lax.fori_loop(0, chunks, last_frame, 0)
+
+        @pl.when(step == 3)
+        def _():
+            def high_frame(i, carry):
+                at = spot(i)
+                f0 = planes[(0,) + at]
+                o1 = planes[(kept,) + at] - 0.5 * (f0 + planes[(2,) + at])
+                result[(kept,) + at] = o1
+                planes[(kept,) + at] = f0 + 0.25 * o1
+
+                @pl.when(both(is_left, no(is_first)))
+                def _():
+                    far(1, i, planes.at[(kept,) + spot(i)]).start()
+
+                return carry
+
+            lax.fori_loop(0, chunks, high_frame, 0)
+
+            def high_group(g, carry):
+                c = phase_at(PAIRED + g)
+                o1 = planes[kept, c] - 0.5 * (planes[kept - 1, c] + planes[kept + 1, c])
+                planes[kept, c] = o1
+                result[kept, c] = o1
+                start_forward(kept, g)
+                return carry
+
+            lax.fori_loop(0, grouped, high_group, 0)
+
+        @pl.when(step == 1)
+        def _():
+            relay_some(straight, straight + 3)
+
+        @pl.when(step == 2)
+        def _():
+            relay_some(straight + 3, straight + 8)
 
         return carry
 
     lax.fori_loop(0, frames, one_frame, 0)
+    acc[...] = jnp.zeros_like(acc)
+
     total = GROUP * frames
 
-    def send_halo(q):
-        c = phase_at(q)
+    def send_halo(c):
         arrived(held.at[pl.ds(0, total - frames), c], f_recv.at[c])
         arrived(held.at[pl.ds(0, frames), c], f_own.at[c])
 
@@ -464,8 +612,7 @@
         lax.fori_loop(0, width // LANES, strip, 0)
         start_halos(c)
 
-    def finish(q):
-        c = phase_at(q)
+    def finish(c):
         halo_arrivals(c)
 
         def strip(i, carry):
@@ -473,7 +620,7 @@
             f = [held[n, c, :, lanes] for n in range(total)]
             before = [from_before[c, j, :, lanes] for j in range(TLEVELS)]
             after = [from_after[c, j, :, lanes] for j in range(TLEVELS)]
-            out = temporal(f, before, after, is_first, is_last)
+            out = temporal(f, before, after, starts, ends)
             sums = [None] * (TLEVELS + 1)
             for n in range(total):
                 if n % frames in moved:
@@ -489,21 +636,216 @@
         zero = jnp.zeros((8, LANES), jnp.float32)
         sums = lax.fori_loop(0, width // LANES, strip, (zero,) * (TLEVELS + 1))
         for t in range(TLEVELS + 1):
-            acc[c, t] = sums[t]
+            acc[phase_at(PAIRED + c), t] = sums[t]
+        for i in range(len(moved)):
+            back_own(i, c).start()
+
+    def give_back(c):
         for i in range(len(moved)):
             for k in range(GROUP - 1):
                 back(i, c, k).start()
-            back_own(i, c).start()
-
-    send_halo(0)
-
-    def middle(q, carry):
-        send_halo(q)
-        finish(q - 1)
-        return carry
-
-    lax.fori_loop(1, phases, middle, 0)
-    finish(phases - 1)
+
+    def count_in(n, t, i):
+        c, rows = spot(i)
+        value = result[n, c, rows, :]
+        square = value * value
+        folded = sum(square[:, k : k + LANES] for k in range(0, width, LANES))
+        acc[c, t] += jnp.sum(folded.reshape(cut // 8, 8, LANES), axis=0)
+
+    def loop(start, stop, body):
+        def step(i, carry):
+            body(i)
+            return carry
+
+        lax.fori_loop(start, stop, step, 0)
+
+    lag = 4
+
+    def halves(i):
+        at = spot(i)
+        return planes[(2,) + at], result[(1,) + at], result[(3,) + at], planes[(1,) + at]
+
+    def third(i, after):
+        at = spot(i)
+        result[(3,) + at] = planes[(3,) + at] - 0.5 * after
+
+    @pl.when(is_left)
+    def _():
+        def highs(i):
+            third(i, take_near(0, i))
+
+        def relays(i):
+            @pl.when(no(is_last))
+            def _():
+                relay(i, 0)
+
+        def questions(i):
+            o3 = result[(3,) + spot(i)]
+            made[(1,) + slot(i)] = 0.25 * o3
+
+            @pl.when(no(is_last))
+            def _():
+                made[(1,) + slot(i)] = 0.25 * result[(3,) + spot(i)] + take_far(1, i)
+
+            near(1, i, made.at[(1,) + slot(i)]).start()
+
+        ahead = straight + 12
+        loop(straight + 8, ahead, relays)
+        loop(0, chunks - ahead, lambda i: (relays(i + ahead), highs(i)))
+        loop(chunks - ahead, chunks, highs)
+        loop(0, chunks, questions)
+
+    @pl.when(is_right)
+    def _():
+        def highs(i):
+            at = spot(i)
+
+            @pl.when(is_last)
+            def _():
+                third(i, planes[(2,) + at])
+
+            @pl.when(no(is_last))
+            def _():
+                third(i, take_near(0, i))
+
+        def answer_highs(i):
+            made[(0,) + slot(i)] = planes[(1,) + spot(i)]
+
+            @pl.when(no(is_first))
+            def _():
+                made[(0,) + slot(i)] = planes[(1,) + spot(i)] + 0.25 * take_far(0, i)
+
+            near(1, i, made.at[(0,) + slot(i)]).start()
+
+        def highs_and_answers(i):
+            highs(i)
+            answer_highs(i - lag)
+
+        loop(0, lag, highs)
+        loop(lag, chunks, highs_and_answers)
+        loop(chunks - lag, chunks, answer_highs)
+
+    loop(0, grouped, send_halo)
+
+    def left_seconds(i):
+        at = spot(i)
+        f2, o1, o3, h = halves(i)
+        start = jnp.where(is_first, 0.125 * o1, -0.0625 * planes[(0,) + at])
+        p2 = f2 + 0.25 * (o1 + o3) - 0.5 * h - 0.125 * o3 - start
+        p2 = p2 - 0.5 * take_near(1, i)
+        result[(2,) + at] = p2
+        made[(2,) + slot(i)] = h + 0.25 * p2
+
+        @pl.when(no(is_first))
+        def _():
+            far(2, i, made.at[(2,) + slot(i)]).start()
+
+    def right_seconds(i):
+        at = spot(i)
+        f2, o1, o3, h = halves(i)
+        came = take_near(1, i)
+        p2 = f2 + 0.25 * (o1 + o3)
+        p2 = p2 - jnp.where(is_last, h + came, 0.5 * (h + came) + 0.125 * o3)
+        result[(2,) + at] = p2
+        made[(1,) + slot(i)] = 0.25 * (o3 + p2)
+
+        @pl.when(no(is_last))
+        def _():
+            far(1, i, made.at[(1,) + slot(i)]).start()
+
+    def seconds(j):
+        @pl.when(is_left)
+        def _():
+            loop(j * CUTS, (j + 1) * CUTS, left_seconds)
+
+        @pl.when(is_right)
+        def _():
+            loop(j * CUTS, (j + 1) * CUTS, right_seconds)
+
+    loop(0, PAIRED, seconds)
+    loop(0, grouped, finish)
+
+    @pl.when(is_left)
+    def _():
+        def thirds(i):
+            f2, o1, o3, h = halves(i)
+            p2 = result[(2,) + spot(i)]
+            own = 0.25 * (o3 + p2) - jnp.where(is_last, 1.0, 0.5) * made[(2,) + slot(i)]
+            made[(3,) + slot(i)] = own - jnp.where(is_first, 0.125, 0.0) * (o1 + p2)
+
+            @pl.when(no(is_last))
+            def _():
+                made[(3,) + slot(i)] -= 0.5 * take_far(2, i)
+
+            near(2, i, made.at[(3,) + slot(i)]).start()
+
+        loop(0, 0, give_back)
+        loop(0, chunks, thirds)
+        loop(0, grouped, give_back)
+
+        def sums_so_far(i):
+            count_in(1, 0, i)
+            count_in(3, 0, i)
+            count_in(2, 1, i)
+
+        loop(0, chunks, sums_so_far)
+
+        def lows(i):
+            at = spot(i)
+            start = jnp.where(is_first, 0.25, 0.0) * (result[(1,) + at] + result[(2,) + at])
+            result[(0,) + at] = made[(2,) + slot(i)] + start + take_near(2, i)
+            count_in(0, 3, i)
+
+        loop(0, chunks, lows)
+
+    @pl.when(is_right)
+    def _():
+        def thirds(i):
+            at = spot(i)
+            mine = made[(1,) + slot(i)]
+            scale = jnp.where(is_last, 0.0, 0.5)
+            result[(0,) + at] = (
+                planes[(1,) + at] + 0.25 * result[(2,) + at] - scale * mine
+            )
+
+            @pl.when(no(is_first))
+            def _():
+                result[(0,) + at] -= jnp.where(is_last, 1.0, 0.5) * take_far(1, i)
+
+            d = result[(0,) + at] + take_near(2, i)
+            result[(0,) + at] = d
+            made[(2,) + slot(i)] = mine + 0.25 * d
+
+            @pl.when(no(is_last))
+            def _():
+                far(2, i, made.at[(2,) + slot(i)]).start()
+
+        def answer_thirds(i):
+            made[(3,) + slot(i)] = jnp.where(is_first, 0.5, 0.25) * result[(0,) + spot(i)]
+
+            @pl.when(no(is_first))
+            def _():
+                made[(3,) + slot(i)] += take_far(2, i)
+
+            near(2, i, made.at[(3,) + slot(i)]).start()
+
+        def thirds_and_answers(i):
+            thirds(i)
+            answer_thirds(i - lag)
+
+        loop(0, 1, give_back)
+        loop(0, lag, thirds)
+        loop(lag, chunks, thirds_and_answers)
+        loop(chunks - lag, chunks, answer_thirds)
+        loop(1, grouped, give_back)
+
+        def all_sums(i):
+            count_in(1, 0, i)
+            count_in(3, 0, i)
+            count_in(2, 1, i)
+            count_in(0, 2, i)
+
+        loop(0, chunks, all_sums)
 
     lane = lax.broadcasted_iota(jnp.int32, (1, LANES), 1)
     packed[...] = jnp.zeros_like(packed)
@@ -544,20 +886,45 @@
         sums, band, precision=lax.Precision.HIGHEST, preferred_element_type=jnp.float32
     )
 
+    arrived(inbox.at[pl.ds(0, all_devices - 1)], s_send)
     for k in range(GROUP - 1):
         arrived(held.at[pl.ds(0, frames)], f_send.at[k])
         arrived(held.at[pl.ds(0, len(moved))], r_send.at[k])
         arrived(held.at[pl.ds(0, len(moved))], r_recv.at[k])
     arrived(held.at[pl.ds(0, len(moved))], r_own)
-    arrived(inbox.at[pl.ds(0, all_devices - 1)], s_send)
-
-    @pl.when(jnp.logical_not(is_first))
+
+    @pl.when(jnp.logical_not(starts))
     def _():
         arrived(to_before, h_send.at[0])
 
-    @pl.when(jnp.logical_not(is_last))
+    @pl.when(jnp.logical_not(ends))
     def _():
         arrived(to_after, h_send.at[1])
+
+    for kind in (1, 2):
+        arrived(near_in.at[kind], n_send.at[kind])
+
+    @pl.when(is_right)
+    def _():
+        arrived(near_in.at[0], n_send.at[0])
+
+    @pl.when(both(is_left, no(is_last)))
+    def _():
+        arrived(near_in.at[0, pl.ds(0, PAIRED - DIRECT)], n_send.at[0])
+
+    @pl.when(jnp.logical_or(both(is_left, no(is_first)), both(is_right, no(is_last))))
+    def _():
+        for kind in (1, 2):
+            arrived(far_in.at[kind], p_send.at[kind])
+
+    @pl.when(both(is_left, no(is_first)))
+    def _():
+        arrived(near_in.at[0, pl.ds(0, DIRECT)], d_send)
+        arrived(far_in.at[0, pl.ds(0, PAIRED - DIRECT)], p_send.at[0])
+
+    @pl.when(both(is_right, no(is_last)))
+    def _():
+        arrived(far_in.at[0], p_send.at[0])
 
     @pl.when(jnp.logical_not(at_bottom))
     def _():
@@ -581,13 +948,16 @@
     frames, rows, width = footage.shape
     inner = rows // PERIOD
     groups = inner + 2 * MARGIN
-    part = inner // GROUP
     strips = lax.axis_size("row")
     devices = lax.axis_size("frame") * strips
     any_space = pl.BlockSpec(memory_space=pl.ANY)
     vmem = pl.BlockSpec(memory_space=pltpu.VMEM)
     f32, bf16 = jnp.float32, jnp.bfloat16
-    halo_buffer = pltpu.VMEM((PERIOD, TLEVELS, part, width), f32)
+    traffic = pltpu.VMEM((3, PAIRED, inner, width), f32)
+    chunks = PAIRED * CUTS
+    grouped = PERIOD - PAIRED
+    part = inner // GROUP
+    halo_buffer = pltpu.VMEM((grouped, TLEVELS, part, width), f32)
     dma = pltpu.SemaphoreType.DMA
     planes, energy = pl.pallas_call(
         video_kernel,
@@ -606,20 +976,24 @@
             pltpu.VMEM((SLEVELS, 2, 2 * BLOCK, BLOCK), bf16),
             pltpu.VMEM((SLEVELS, 2, BLOCK + LANES, BLOCK), bf16),
             pltpu.VMEM((SLEVELS, 2, BLOCK + LANES, BLOCK), bf16),
-            pltpu.VMEM((GROUP * frames, PERIOD, part, width), f32),
+            traffic,
+            traffic,
+            pltpu.VMEM((4, PAIRED, inner, width), f32),
+            pltpu.VMEM((GROUP * frames, grouped, part, width), f32),
             halo_buffer, halo_buffer, halo_buffer, halo_buffer,
             pltpu.VMEM((PERIOD, TLEVELS + 1, 8, LANES), f32),
             pltpu.VMEM((8, LANES), f32),
             pltpu.VMEM((devices, 8, LANES), f32),
             dma((frames,)), dma((SLEVELS, 3)),
             dma((2,)), dma((2, frames)),
-            dma((GROUP - 1,)), dma((PERIOD,)), dma((PERIOD,)),
-            dma((2,)), dma((2, PERIOD)),
+            dma((3,)), dma((3, chunks)), dma((3,)), dma((3, chunks)), dma,
+            dma((GROUP - 1,)), dma((grouped,)), dma((grouped,)),
+            dma((2,)), dma((2, grouped)),
             dma((GROUP - 1,)), dma((GROUP - 1,)), dma,
             dma, dma,
         ],
         compiler_params=pltpu.CompilerParams(
-            collective_id=0, has_side_effects=True, vmem_limit_bytes=40 * 2**20
+            collective_id=0, has_side_effects=True, vmem_limit_bytes=44 * 2**20
         ),
     )(
         footage.reshape(frames, inner, PERIOD, width),

time: 179 us -> 177 us (0.989)
  Pallas kernels: 177 us -> 173 us
    pallas_call x1, Pallas kernels: 173 us -> 169 us  [shards(): pl.pallas_call(video_kernel, out_shape=(jax.ShapeDtypeStruct((frames, PER...]
where the time goes in v3:
time: 177 us; the launch traced here: 175 us
  Pallas kernels  173 us (98%)
    pallas_call x1, Pallas kernels, shards(): pl.pallas_call(video_kernel, out_shape=(jax.ShapeDtypeStruct((frames, PER...  169 us
    pallas_call x1, Pallas kernels, shards(): pl.pallas_call(weave_kernel, out_shape=(jax.ShapeDtypeStruct((frames, inn...  3.84 us

profile of v3, /device:TPU:0, one launch (start us, length us, event | category | flops | bytes accessed | tf_op | source)
XLA Modules:
  0.0 175.3 jit_solution(16847672151938164771)
XLA Ops:
  0.6 0.0 copy-start
  0.6 1.5 copy-done
  2.2 169.2 %shard_map.41 = (f32[4,8,64,1024]{3,2,1,0:T(8,128)S(1)}, f32[8,128]{1,0:T(8,128)S(1)}) custom-call(f32[4,64,8,1024]{3,2,1,0:T(8,128)} %bitcast.2, bf16[3,2,640,256]{3,2,1,0:T(8,128)(2,1)S(1)} %copy-done), custom_call_target="tpu_custom_call" | custom-call | tf_op jit(solution)/shard_map/pallas_call | solution.py:962
  171.4 3.8 %shard_map.42 = (f32[4,64,8,1024]{3,2,1,0:T(8,128)}, f32[4,10]{1,0:T(4,128)}) custom-call(f32[4,8,64,1024]{3,2,1,0:T(8,128)S(1)} %get-tuple-element.6.planes, f32[8,128]{1,0:T(8,128)S(1)} %get-tuple-element.7.energy), custom_call_target="tpu_custom_call" | custom-call | tf_op jit(solution)/shard_map/pallas_call | solution.py:1002
Async XLA Ops:
  0.6 1.5 copy-start

commit v4 on v3

--- a/solution.py
+++ b/solution.py
@@ -584,11 +584,11 @@
 
         @pl.when(step == 1)
         def _():
-            relay_some(straight, straight + 3)
+            relay_some(straight, straight + 4)
 
         @pl.when(step == 2)
         def _():
-            relay_some(straight + 3, straight + 8)
+            relay_some(straight + 4, straight + 10)
 
         return carry
 
@@ -689,8 +689,8 @@
 
             near(1, i, made.at[(1,) + slot(i)]).start()
 
-        ahead = straight + 12
-        loop(straight + 8, ahead, relays)
+        ahead = straight + 14
+        loop(straight + 10, ahead, relays)
         loop(0, chunks - ahead, lambda i: (relays(i + ahead), highs(i)))
         loop(chunks - ahead, chunks, highs)
         loop(0, chunks, questions)
@@ -765,6 +765,11 @@
     loop(0, PAIRED, seconds)
     loop(0, grouped, finish)
 
+    def sums_so_far(i):
+        count_in(1, 0, i)
+        count_in(3, 0, i)
+        count_in(2, 1, i)
+
     @pl.when(is_left)
     def _():
         def thirds(i):
@@ -782,11 +787,6 @@
         loop(0, 0, give_back)
         loop(0, chunks, thirds)
         loop(0, grouped, give_back)
-
-        def sums_so_far(i):
-            count_in(1, 0, i)
-            count_in(3, 0, i)
-            count_in(2, 1, i)
 
         loop(0, chunks, sums_so_far)
 
@@ -814,6 +814,7 @@
 
             d = result[(0,) + at] + take_near(2, i)
             result[(0,) + at] = d
+            count_in(0, 2, i)
             made[(2,) + slot(i)] = mine + 0.25 * d
 
             @pl.when(no(is_last))
@@ -834,18 +835,11 @@
             answer_thirds(i - lag)
 
         loop(0, 1, give_back)
+        loop(0, chunks, sums_so_far)
         loop(0, lag, thirds)
         loop(lag, chunks, thirds_and_answers)
         loop(chunks - lag, chunks, answer_thirds)
         loop(1, grouped, give_back)
-
-        def all_sums(i):
-            count_in(1, 0, i)
-            count_in(3, 0, i)
-            count_in(2, 1, i)
-            count_in(0, 2, i)
-
-        loop(0, chunks, all_sums)
 
     lane = lax.broadcasted_iota(jnp.int32, (1, LANES), 1)
     packed[...] = jnp.zeros_like(packed)

time: 177 us -> 177 us (level)
  no operation moved by 1% of the time
where the time goes in v4:
time: 177 us; the launch traced here: 175 us
  Pallas kernels  173 us (98%)
    pallas_call x1, Pallas kernels, shards(): pl.pallas_call(video_kernel, out_shape=(jax.ShapeDtypeStruct((frames, PER...  169 us
    pallas_call x1, Pallas kernels, shards(): pl.pallas_call(weave_kernel, out_shape=(jax.ShapeDtypeStruct((frames, inn...  3.84 us

profile of v4, /device:TPU:0, one launch (start us, length us, event | category | flops | bytes accessed | tf_op | source)
XLA Modules:
  0.0 175.3 jit_solution(4074059955798863894)
XLA Ops:
  0.6 0.0 copy-start
  0.6 1.5 copy-done
  2.2 169.2 %shard_map.41 = (f32[4,8,64,1024]{3,2,1,0:T(8,128)S(1)}, f32[8,128]{1,0:T(8,128)S(1)}) custom-call(f32[4,64,8,1024]{3,2,1,0:T(8,128)} %bitcast.2, bf16[3,2,640,256]{3,2,1,0:T(8,128)(2,1)S(1)} %copy-done), custom_call_target="tpu_custom_call" | custom-call | tf_op jit(solution)/shard_map/pallas_call | solution.py:956
  171.4 3.8 %shard_map.42 = (f32[4,64,8,1024]{3,2,1,0:T(8,128)}, f32[4,10]{1,0:T(4,128)}) custom-call(f32[4,8,64,1024]{3,2,1,0:T(8,128)S(1)} %get-tuple-element.6.planes, f32[8,128]{1,0:T(8,128)S(1)} %get-tuple-element.7.energy), custom_call_target="tpu_custom_call" | custom-call | tf_op jit(solution)/shard_map/pallas_call | solution.py:996
Async XLA Ops:
  0.6 1.5 copy-start
